TPU v7x, 128 devices: a whole 4x4x4 slice. The times are simulated.
128 devices in a mesh: ccy: 4 (over z_lo, core), path: 32 (over y, x, z_hi).
Axes of the slice: x: 4, y: 4, z: 4 (z_hi: 2, z_lo: 2; z = z_hi * 2 + z_lo), core: 2. Of those that a mesh axis runs over, the one named last changes fastest.
Arguments:
- curve_store: bfloat16 [4, 64, 64, 8192], P('ccy', 'path'), may hold values from -0.13 to 0.18
- cash_index: int32 [4, 2048, 16], P('ccy'), may hold values from 0 to 1023
- cash_amount: float32 [4, 2048, 16], P('ccy'), may hold values from -0.6 to 0.6
- trade_set: int32 [4, 2048], P('ccy'), may hold values from 0 to 511
- date_slot: int32 [16], replicated, may hold values from 0 to 63, as said below
- default_weight: float32 [16, 512], replicated, may hold values from 0.02 to 0.2
Outputs:
- exposure: float32 [16, 512], P(None, 'ccy')
- node_sens: float32 [4, 16, 64], P('ccy')
Inputs may be any that keep to these rules, and one draw needn't show every extreme that they name: `date_slot`: the 16 slots are distinct; slot s is stored at path index s // 2, position s % 2.
All inputs are finite; a program needn't handle non-finite values.
Results may differ from a plain program's by a relative error of at most 0.0029.
Values may be sent and summed in bfloat16 or wider, within the bound.
A program may use at most 64 MiB of HBM per device.

v0:
```python
import jax
import jax.numpy as jnp
from jax import lax
from jax.sharding import PartitionSpec as P

NODES = 64
CFG = 1024
NSETS = 512
DATES = 16
PATHS_DEV = 256


SOFTEN = 0.04
HORIZON = 32.0


def cut_along(array, dim, devices):
    shape = array.shape
    pieces = array.reshape(*shape[:dim], devices, shape[dim] // devices, *shape[dim + 1 :])
    return jnp.moveaxis(pieces, dim, 0)


def piece_ends(length, count):
    unit = 8 if length >= 8 * count else 1
    return [length // unit * k // count * unit for k in range(1, count)]


def laid_out(pieces, dim):
    shape = list(pieces.shape[1:])
    shape[dim] *= pieces.shape[0]
    return jnp.moveaxis(pieces, 0, dim).reshape(shape)


def cut_exchange(array, axis, pieces, split_dim, concat_dim):
    blocks = cut_along(array, split_dim, lax.axis_size(axis))
    widest = max(range(1, max(2, blocks.ndim - 1)), key=lambda d: blocks.shape[d])
    finished = []
    for share in jnp.split(blocks, piece_ends(blocks.shape[widest], pieces), axis=widest):
        if share.size:
            finished.append(lax.all_to_all(share, axis, split_axis=0, concat_axis=0, tiled=True))
    return laid_out(jnp.concatenate(finished, axis=widest), concat_dim)


def from_everyone(array, axis):
    copies = jnp.broadcast_to(array, (lax.axis_size(axis), *array.shape))
    return lax.all_to_all(copies, axis, split_axis=0, concat_axis=0, tiled=True)


def over_copies(array, axis):
    return from_everyone(array, axis).sum(axis=0)


def together(arrays, axis):
    ends = [0]
    for a in arrays:
        ends.append(ends[-1] + a.size)
    total = over_copies(jnp.concatenate([a.ravel() for a in arrays]), axis)
    return tuple((total[b:e].reshape(a.shape) for a, b, e in zip(arrays, ends, ends[1:])))


def date_tables(date_index, node_count, grid_count):
    start_time = 0.5 * (jnp.asarray(date_index).astype(jnp.float32) + 1.0)
    grid_times = HORIZON * (jnp.arange(grid_count, dtype=jnp.float32) + 1.0) / grid_count
    tenors = HORIZON * (jnp.arange(node_count, dtype=jnp.float32) + 1.0) / node_count
    remain = grid_times - start_time
    alive_mask = (remain > 0.0).astype(jnp.float32)
    clipped = jnp.clip(remain, HORIZON / node_count, HORIZON)
    weights = jnp.maximum(
        0.0, 1.0 - jnp.abs(clipped[None, :] - tenors[:, None]) * (node_count / HORIZON)
    )
    return (remain, alive_mask, weights)


def netted_cash(flow_index, amount, trade_sets):
    columns = jnp.repeat(trade_sets, flow_index.shape[1])
    cash_table = (
        jnp.zeros((CFG, NSETS), jnp.float32)
        .at[flow_index.reshape(-1), columns]
        .add(amount.reshape(-1))
    )
    return cash_table.astype(jnp.bfloat16)


def local(curve_store, cash_index, cash_amount, trade_set, date_slot, default_weight):
    groups = lax.axis_size("ccy")
    group_index = lax.axis_index("ccy")
    share_size = NSETS // groups
    total_paths = PATHS_DEV * lax.axis_size("path")
    cash_table = netted_cash(cash_index[0], cash_amount[0], trade_set[0])
    blocks = cut_exchange(curve_store, "path", 2, 3, 1)[0]
    cash_all = lax.all_gather(cash_table[None], "ccy", axis=0, tiled=True)

    def fetch_curve(slot_id):
        found = lax.dynamic_index_in_dim(blocks, slot_id, 0, keepdims=False)
        return found

    def advance(unused, inputs):
        date_index, slot_id, weight_row = inputs
        remain, alive_mask, weights = date_tables(date_index, NODES, CFG)
        grid_weights = weights.astype(jnp.bfloat16)
        curve_now = fetch_curve(slot_id)
        curve_groups = lax.all_gather(curve_now[None], "ccy", axis=0, tiled=True)
        yields = jnp.einsum(
            "gnp,nc->gpc", curve_groups, grid_weights, preferred_element_type=jnp.float32
        )
        discount_all = alive_mask * jnp.exp(-yields * remain)
        values = jnp.einsum(
            "gpc,gcs->ps",
            discount_all.astype(jnp.bfloat16),
            cash_all,
            preferred_element_type=jnp.float32,
        )
        discount = lax.dynamic_index_in_dim(discount_all, group_index, 0, keepdims=False)
        rooted = jnp.sqrt(values * values + SOFTEN)
        slopes = (weight_row / total_paths * 0.5 * (1.0 + values / rooted)).astype(jnp.bfloat16)
        share_values = lax.dynamic_slice_in_dim(values, group_index * share_size, share_size, 1)
        share_root = lax.dynamic_slice_in_dim(rooted, group_index * share_size, share_size, 1)
        exposure_part = jnp.sum(0.5 * (share_values + share_root), axis=0) / total_paths
        back_flow = lax.dot_general(
            slopes, cash_table, (((1,), (1,)), ((), ())), preferred_element_type=jnp.float32
        )
        node_pull = jnp.sum(back_flow * -remain * discount, axis=0)
        sens_part = jnp.dot(weights, node_pull, precision=lax.Precision.HIGHEST)
        return (unused, (exposure_part, sens_part))

    inputs = (jnp.arange(DATES, dtype=jnp.int32), date_slot, default_weight)
    unused, (exposure_rows, sens_rows) = lax.scan(advance, jnp.zeros((), jnp.float32), inputs)
    exposure_rows, sens_rows = together((exposure_rows, sens_rows), "path")
    return (exposure_rows, sens_rows[None])


def solution(mesh):
    in_specs = (
        P("ccy", "path", None, None),
        P("ccy", None, None),
        P("ccy", None, None),
        P("ccy", None),
        P(),
        P(),
    )
    out_specs = (P(None, "ccy"), P("ccy", None, None))
    return jax.shard_map(local, mesh=mesh, in_specs=in_specs, out_specs=out_specs, check_vma=False)
```

profile of v0, /device:TPU:1, one launch (start us, length us, event | category | flops | bytes accessed | tf_op | source)
XLA Modules:
  0.0 543.9 jit_solution(14642358326051136279)
XLA Ops:
  12.4 171.6 %scatter_custom_fusion = f32[524288]{0:T(1024)S(1)} fusion(s32[32768]{0:T(1024)S(1)} %broadcast_select_fusion, f32[32768]{0:T(1024)S(1)} %reshape.152, f32[]{:T(128)} %constant.138.clone.1), kind=kCustom, calls=%fused_computation.44 | custom fusion | flops 32768 | bytes 2097156
  184.1 1.5 broadcast_in_dim.41
  186.9 1.6 copy.23
  188.4 11.2 %all-to-all-start.1 = ((bf16[32,1,2,32,256]{4,3,2,1,0:T(8,128)(2,1)}), bf16[32,1,2,32,256]{4,3,2,1,0:T(8,128)(2,1)S(1)}, u32[]{:S(2)}, u32[]{:S(2)}) async-start(bf16[32,1,2,32,256]{4,3,2,1,0:T(8,128)(2,1)} %copy.23), calls=%async_computation.1 | async-start | bytes 2097152 | tf_op jit(solution)/shard_map/all_to_all | solution.py:40
  199.6 1.6 copy.22
  201.2 16.8 %all-to-all-done.1 = bf16[32,1,2,32,256]{4,3,2,1,0:T(8,128)(2,1)S(1)} async-done(((bf16[32,1,2,32,256]{4,3,2,1,0:T(8,128)(2,1)}), bf16[32,1,2,32,256]{4,3,2,1,0:T(8,128)(2,1)S(1)}, u32[]{:S(2)}, u32[]{:S(2)}) %all-to-all-start.1) | async-done | bytes 1048608 | tf_op jit(solution)/shard_map/all_to_all | solution.py:40
  218.0 3.9 all-to-all-start
  221.9 1.5 reshape.148
  223.4 16.0 %all-to-all-done = bf16[32,1,2,32,256]{4,3,2,1,0:T(8,128)(2,1)S(1)} async-done(((bf16[32,1,2,32,256]{4,3,2,1,0:T(8,128)(2,1)}), bf16[32,1,2,32,256]{4,3,2,1,0:T(8,128)(2,1)S(1)}, u32[]{:S(2)}, u32[]{:S(2)}) %all-to-all-start) | async-done | bytes 1048608 | tf_op jit(solution)/shard_map/all_to_all | solution.py:40
  239.4 1.6 pad_maximum_fusion
  241.0 17.1 %all-gather.2.cloned.1.call-done = bf16[4,1024,512]{2,1,0:T(8,128)(2,1)} async-done(((bf16[1,1024,512]{2,1,0:T(8,128)(2,1)}), bf16[4,1024,512]{2,1,0:T(8,128)(2,1)}) %all-gather.2.cloned.1.call-update) | async-done | bytes 4194320 | tf_op jit(solution)/shard_map/all_gather | solution.py:91
  258.1 255.7 %while.15 = (s32[]{:T(128)}, f32[16,128]{1,0:T(8,128)S(1)}, f32[16,64]{1,0:T(8,128)S(1)}, s32[16]{0:T(128)S(1)}, s32[16]{0:T(128)S(1)}, /*index=5*/bf16[64,64,25...) while((s32[]{:T(128)}, f32[16,128]{1,0:T(8,128)S(1)}, ...), condition=%wide.region_4.5_spmd, body=%wide.region_1.4_spmd.sunk | while | flops 1484042880 | bytes 54679916 | solution.py:127
  261.3 5.3 all_gather.12
  271.5 1.8 fusion.54
  277.0 5.5 %all_gather.12 = bf16[4,64,256]{2,1,0:T(8,128)(2,1)S(1)} all-gather(bf16[1,64,256]{2,1,0:T(8,128)(2,1)S(1)} %constant_dynamic-slice_fusion.2), channel_id=1, replica_groups=mesh['ccy'=4,'path'=32] {'ccy'}, dimensions={0}, use_global_device_ids=true | all-gather | bytes 163840 | tf_op jit(solution)/shard_map/while/body/eval_jaxpr/all_gather | solution.py:102
  287.5 1.8 fusion.54
  293.0 5.5 %all_gather.12 = bf16[4,64,256]{2,1,0:T(8,128)(2,1)S(1)} all-gather(bf16[1,64,256]{2,1,0:T(8,128)(2,1)S(1)} %constant_dynamic-slice_fusion.2), channel_id=1, replica_groups=mesh['ccy'=4,'path'=32] {'ccy'}, dimensions={0}, use_global_device_ids=true | all-gather | bytes 163840 | tf_op jit(solution)/shard_map/while/body/eval_jaxpr/all_gather | solution.py:102
  300.7 1.3 add_sqrt_fusion.3
  303.5 1.8 fusion.54
  309.0 5.5 %all_gather.12 = bf16[4,64,256]{2,1,0:T(8,128)(2,1)S(1)} all-gather(bf16[1,64,256]{2,1,0:T(8,128)(2,1)S(1)} %constant_dynamic-slice_fusion.2), channel_id=1, replica_groups=mesh['ccy'=4,'path'=32] {'ccy'}, dimensions={0}, use_global_device_ids=true | all-gather | bytes 163840 | tf_op jit(solution)/shard_map/while/body/eval_jaxpr/all_gather | solution.py:102
  319.5 1.8 fusion.54
  325.0 5.5 %all_gather.12 = bf16[4,64,256]{2,1,0:T(8,128)(2,1)S(1)} all-gather(bf16[1,64,256]{2,1,0:T(8,128)(2,1)S(1)} %constant_dynamic-slice_fusion.2), channel_id=1, replica_groups=mesh['ccy'=4,'path'=32] {'ccy'}, dimensions={0}, use_global_device_ids=true | all-gather | bytes 163840 | tf_op jit(solution)/shard_map/while/body/eval_jaxpr/all_gather | solution.py:102
  335.5 1.8 fusion.54
  341.0 5.5 %all_gather.12 = bf16[4,64,256]{2,1,0:T(8,128)(2,1)S(1)} all-gather(bf16[1,64,256]{2,1,0:T(8,128)(2,1)S(1)} %constant_dynamic-slice_fusion.2), channel_id=1, replica_groups=mesh['ccy'=4,'path'=32] {'ccy'}, dimensions={0}, use_global_device_ids=true | all-gather | bytes 163840 | tf_op jit(solution)/shard_map/while/body/eval_jaxpr/all_gather | solution.py:102
  351.5 1.8 fusion.54
  357.0 5.5 %all_gather.12 = bf16[4,64,256]{2,1,0:T(8,128)(2,1)S(1)} all-gather(bf16[1,64,256]{2,1,0:T(8,128)(2,1)S(1)} %constant_dynamic-slice_fusion.2), channel_id=1, replica_groups=mesh['ccy'=4,'path'=32] {'ccy'}, dimensions={0}, use_global_device_ids=true | all-gather | bytes 163840 | tf_op jit(solution)/shard_map/while/body/eval_jaxpr/all_gather | solution.py:102
  364.7 1.3 add_sqrt_fusion.3
  367.5 1.8 fusion.54
  373.0 5.5 %all_gather.12 = bf16[4,64,256]{2,1,0:T(8,128)(2,1)S(1)} all-gather(bf16[1,64,256]{2,1,0:T(8,128)(2,1)S(1)} %constant_dynamic-slice_fusion.2), channel_id=1, replica_groups=mesh['ccy'=4,'path'=32] {'ccy'}, dimensions={0}, use_global_device_ids=true | all-gather | bytes 163840 | tf_op jit(solution)/shard_map/while/body/eval_jaxpr/all_gather | solution.py:102
  383.5 1.8 fusion.54
  389.0 5.5 %all_gather.12 = bf16[4,64,256]{2,1,0:T(8,128)(2,1)S(1)} all-gather(bf16[1,64,256]{2,1,0:T(8,128)(2,1)S(1)} %constant_dynamic-slice_fusion.2), channel_id=1, replica_groups=mesh['ccy'=4,'path'=32] {'ccy'}, dimensions={0}, use_global_device_ids=true | all-gather | bytes 163840 | tf_op jit(solution)/shard_map/while/body/eval_jaxpr/all_gather | solution.py:102
  399.5 1.8 fusion.54
  405.0 5.5 %all_gather.12 = bf16[4,64,256]{2,1,0:T(8,128)(2,1)S(1)} all-gather(bf16[1,64,256]{2,1,0:T(8,128)(2,1)S(1)} %constant_dynamic-slice_fusion.2), channel_id=1, replica_groups=mesh['ccy'=4,'path'=32] {'ccy'}, dimensions={0}, use_global_device_ids=true | all-gather | bytes 163840 | tf_op jit(solution)/shard_map/while/body/eval_jaxpr/all_gather | solution.py:102
  415.5 1.8 fusion.54
  421.0 5.5 %all_gather.12 = bf16[4,64,256]{2,1,0:T(8,128)(2,1)S(1)} all-gather(bf16[1,64,256]{2,1,0:T(8,128)(2,1)S(1)} %constant_dynamic-slice_fusion.2), channel_id=1, replica_groups=mesh['ccy'=4,'path'=32] {'ccy'}, dimensions={0}, use_global_device_ids=true | all-gather | bytes 163840 | tf_op jit(solution)/shard_map/while/body/eval_jaxpr/all_gather | solution.py:102
  428.7 1.3 add_sqrt_fusion.3
  431.5 1.8 fusion.54
  437.0 5.5 %all_gather.12 = bf16[4,64,256]{2,1,0:T(8,128)(2,1)S(1)} all-gather(bf16[1,64,256]{2,1,0:T(8,128)(2,1)S(1)} %constant_dynamic-slice_fusion.2), channel_id=1, replica_groups=mesh['ccy'=4,'path'=32] {'ccy'}, dimensions={0}, use_global_device_ids=true | all-gather | bytes 163840 | tf_op jit(solution)/shard_map/while/body/eval_jaxpr/all_gather | solution.py:102
  447.5 1.8 fusion.54
  453.0 5.5 %all_gather.12 = bf16[4,64,256]{2,1,0:T(8,128)(2,1)S(1)} all-gather(bf16[1,64,256]{2,1,0:T(8,128)(2,1)S(1)} %constant_dynamic-slice_fusion.2), channel_id=1, replica_groups=mesh['ccy'=4,'path'=32] {'ccy'}, dimensions={0}, use_global_device_ids=true | all-gather | bytes 163840 | tf_op jit(solution)/shard_map/while/body/eval_jaxpr/all_gather | solution.py:102
  463.5 1.8 fusion.54
  469.0 5.5 %all_gather.12 = bf16[4,64,256]{2,1,0:T(8,128)(2,1)S(1)} all-gather(bf16[1,64,256]{2,1,0:T(8,128)(2,1)S(1)} %constant_dynamic-slice_fusion.2), channel_id=1, replica_groups=mesh['ccy'=4,'path'=32] {'ccy'}, dimensions={0}, use_global_device_ids=true | all-gather | bytes 163840 | tf_op jit(solution)/shard_map/while/body/eval_jaxpr/all_gather | solution.py:102
  479.5 1.8 fusion.54
  485.0 5.5 %all_gather.12 = bf16[4,64,256]{2,1,0:T(8,128)(2,1)S(1)} all-gather(bf16[1,64,256]{2,1,0:T(8,128)(2,1)S(1)} %constant_dynamic-slice_fusion.2), channel_id=1, replica_groups=mesh['ccy'=4,'path'=32] {'ccy'}, dimensions={0}, use_global_device_ids=true | all-gather | bytes 163840 | tf_op jit(solution)/shard_map/while/body/eval_jaxpr/all_gather | solution.py:102
  495.5 1.8 fusion.54
  501.0 5.5 %all_gather.12 = bf16[4,64,256]{2,1,0:T(8,128)(2,1)S(1)} all-gather(bf16[1,64,256]{2,1,0:T(8,128)(2,1)S(1)} %constant_dynamic-slice_fusion.2), channel_id=1, replica_groups=mesh['ccy'=4,'path'=32] {'ccy'}, dimensions={0}, use_global_device_ids=true | all-gather | bytes 163840 | tf_op jit(solution)/shard_map/while/body/eval_jaxpr/all_gather | solution.py:102
  511.5 1.8 fusion.54
  514.1 21.5 %all_to_all.16 = f32[32,1,3072]{2,1,0:T(1,128)S(1)} all-to-all(f32[32,1,3072]{2,1,0:T(1,128)S(1)} %broadcast_in_dim.42), channel_id=1, replica_groups=mesh['ccy'=4,'path'=32] {'path'}, dimensions={0} | all-to-all | bytes 786432 | tf_op jit(solution)/shard_map/all_to_all | solution.py:46
  (368 shorter events, 104.3 us)
Async XLA Ops:
  7.2 3.5 copy-start.5
  7.2 4.1 copy-start.6
  7.2 4.6 copy-start.4
  7.2 250.9 %all-gather.2.cloned.1.call-start = ((), (), s32[]{:S(2)}) async-start(), calls=%async_computation.3 | async-start | bytes 5242880 | tf_op jit(solution)/shard_map/all_gather | solution.py:91
  188.4 29.5 %all-to-all-start.1 = ((bf16[32,1,2,32,256]{4,3,2,1,0:T(8,128)(2,1)}), bf16[32,1,2,32,256]{4,3,2,1,0:T(8,128)(2,1)S(1)}, u32[]{:S(2)}, u32[]{:S(2)}) async-start(bf16[32,1,2,32,256]{4,3,2,1,0:T(8,128)(2,1)} %copy.23), calls=%async_computation.1 | async-start | bytes 2097152 | tf_op jit(solution)/shard_map/all_to_all | solution.py:40
  201.2 56.9 %copy-start.7 = (s32[16]{0:T(128)S(1)}, s32[16]{0:T(128)}, u32[]{:S(2)}) copy-start(s32[16]{0:T(128)} %param.12) | copy-start | bytes 196
  218.0 21.4 %all-to-all-start = ((bf16[32,1,2,32,256]{4,3,2,1,0:T(8,128)(2,1)}), bf16[32,1,2,32,256]{4,3,2,1,0:T(8,128)(2,1)S(1)}, u32[]{:S(2)}, u32[]{:S(2)}) async-start(bf16[32,1,2,32,256]{4,3,2,1,0:T(8,128)(2,1)} %copy.22), calls=%async_computation | async-start | bytes 2097152 | tf_op jit(solution)/shard_map/all_to_all | solution.py:40
  260.4 8.3 %copy-start = (bf16[4,1024,512]{2,1,0:T(8,128)(2,1)S(1)}, bf16[4,1024,512]{2,1,0:T(8,128)(2,1)}, u32[]{:S(2)}) copy-start(bf16[4,1024,512]{2,1,0:T(8,128)(2,1)} %get-tuple-element.333) | copy-start | bytes 12582916 | tf_op jit(solution)/shard_map/while
  268.7 2.0 copy-start.1
  268.7 2.8 copy-start.3
  276.1 8.6 %copy-start = (bf16[4,1024,512]{2,1,0:T(8,128)(2,1)S(1)}, bf16[4,1024,512]{2,1,0:T(8,128)(2,1)}, u32[]{:S(2)}) copy-start(bf16[4,1024,512]{2,1,0:T(8,128)(2,1)} %get-tuple-element.333) | copy-start | bytes 12582916 | tf_op jit(solution)/shard_map/while
  284.7 2.8 copy-start.3
  292.1 8.6 %copy-start = (bf16[4,1024,512]{2,1,0:T(8,128)(2,1)S(1)}, bf16[4,1024,512]{2,1,0:T(8,128)(2,1)}, u32[]{:S(2)}) copy-start(bf16[4,1024,512]{2,1,0:T(8,128)(2,1)} %get-tuple-element.333) | copy-start | bytes 12582916 | tf_op jit(solution)/shard_map/while
  300.7 2.0 copy-start.1
  300.7 2.8 copy-start.3
  308.1 8.6 %copy-start = (bf16[4,1024,512]{2,1,0:T(8,128)(2,1)S(1)}, bf16[4,1024,512]{2,1,0:T(8,128)(2,1)}, u32[]{:S(2)}) copy-start(bf16[4,1024,512]{2,1,0:T(8,128)(2,1)} %get-tuple-element.333) | copy-start | bytes 12582916 | tf_op jit(solution)/shard_map/while
  316.7 2.0 copy-start.1
  316.7 2.8 copy-start.3
  324.1 8.6 %copy-start = (bf16[4,1024,512]{2,1,0:T(8,128)(2,1)S(1)}, bf16[4,1024,512]{2,1,0:T(8,128)(2,1)}, u32[]{:S(2)}) copy-start(bf16[4,1024,512]{2,1,0:T(8,128)(2,1)} %get-tuple-element.333) | copy-start | bytes 12582916 | tf_op jit(solution)/shard_map/while
  332.7 2.0 copy-start.1
  332.7 2.8 copy-start.3
  340.1 8.6 %copy-start = (bf16[4,1024,512]{2,1,0:T(8,128)(2,1)S(1)}, bf16[4,1024,512]{2,1,0:T(8,128)(2,1)}, u32[]{:S(2)}) copy-start(bf16[4,1024,512]{2,1,0:T(8,128)(2,1)} %get-tuple-element.333) | copy-start | bytes 12582916 | tf_op jit(solution)/shard_map/while
  348.7 2.8 copy-start.3
  356.1 8.6 %copy-start = (bf16[4,1024,512]{2,1,0:T(8,128)(2,1)S(1)}, bf16[4,1024,512]{2,1,0:T(8,128)(2,1)}, u32[]{:S(2)}) copy-start(bf16[4,1024,512]{2,1,0:T(8,128)(2,1)} %get-tuple-element.333) | copy-start | bytes 12582916 | tf_op jit(solution)/shard_map/while
  364.7 2.0 copy-start.1
  364.7 2.8 copy-start.3
  372.1 8.6 %copy-start = (bf16[4,1024,512]{2,1,0:T(8,128)(2,1)S(1)}, bf16[4,1024,512]{2,1,0:T(8,128)(2,1)}, u32[]{:S(2)}) copy-start(bf16[4,1024,512]{2,1,0:T(8,128)(2,1)} %get-tuple-element.333) | copy-start | bytes 12582916 | tf_op jit(solution)/shard_map/while
  380.7 2.0 copy-start.1
  380.7 2.8 copy-start.3
  388.1 8.6 %copy-start = (bf16[4,1024,512]{2,1,0:T(8,128)(2,1)S(1)}, bf16[4,1024,512]{2,1,0:T(8,128)(2,1)}, u32[]{:S(2)}) copy-start(bf16[4,1024,512]{2,1,0:T(8,128)(2,1)} %get-tuple-element.333) | copy-start | bytes 12582916 | tf_op jit(solution)/shard_map/while
  396.7 2.0 copy-start.1
  396.7 2.8 copy-start.3
  404.1 8.6 %copy-start = (bf16[4,1024,512]{2,1,0:T(8,128)(2,1)S(1)}, bf16[4,1024,512]{2,1,0:T(8,128)(2,1)}, u32[]{:S(2)}) copy-start(bf16[4,1024,512]{2,1,0:T(8,128)(2,1)} %get-tuple-element.333) | copy-start | bytes 12582916 | tf_op jit(solution)/shard_map/while
  412.7 2.8 copy-start.3
  420.1 8.6 %copy-start = (bf16[4,1024,512]{2,1,0:T(8,128)(2,1)S(1)}, bf16[4,1024,512]{2,1,0:T(8,128)(2,1)}, u32[]{:S(2)}) copy-start(bf16[4,1024,512]{2,1,0:T(8,128)(2,1)} %get-tuple-element.333) | copy-start | bytes 12582916 | tf_op jit(solution)/shard_map/while
  428.7 2.0 copy-start.1
  428.7 2.8 copy-start.3
  436.1 8.6 %copy-start = (bf16[4,1024,512]{2,1,0:T(8,128)(2,1)S(1)}, bf16[4,1024,512]{2,1,0:T(8,128)(2,1)}, u32[]{:S(2)}) copy-start(bf16[4,1024,512]{2,1,0:T(8,128)(2,1)} %get-tuple-element.333) | copy-start | bytes 12582916 | tf_op jit(solution)/shard_map/while
  444.7 2.8 copy-start.3
  452.1 8.6 %copy-start = (bf16[4,1024,512]{2,1,0:T(8,128)(2,1)S(1)}, bf16[4,1024,512]{2,1,0:T(8,128)(2,1)}, u32[]{:S(2)}) copy-start(bf16[4,1024,512]{2,1,0:T(8,128)(2,1)} %get-tuple-element.333) | copy-start | bytes 12582916 | tf_op jit(solution)/shard_map/while
  460.7 2.0 copy-start.1
  460.7 2.8 copy-start.3
  468.1 8.6 %copy-start = (bf16[4,1024,512]{2,1,0:T(8,128)(2,1)S(1)}, bf16[4,1024,512]{2,1,0:T(8,128)(2,1)}, u32[]{:S(2)}) copy-start(bf16[4,1024,512]{2,1,0:T(8,128)(2,1)} %get-tuple-element.333) | copy-start | bytes 12582916 | tf_op jit(solution)/shard_map/while
  476.7 2.8 copy-start.3
  484.1 8.6 %copy-start = (bf16[4,1024,512]{2,1,0:T(8,128)(2,1)S(1)}, bf16[4,1024,512]{2,1,0:T(8,128)(2,1)}, u32[]{:S(2)}) copy-start(bf16[4,1024,512]{2,1,0:T(8,128)(2,1)} %get-tuple-element.333) | copy-start | bytes 12582916 | tf_op jit(solution)/shard_map/while
  492.7 2.8 copy-start.3
  500.1 8.6 %copy-start = (bf16[4,1024,512]{2,1,0:T(8,128)(2,1)S(1)}, bf16[4,1024,512]{2,1,0:T(8,128)(2,1)}, u32[]{:S(2)}) copy-start(bf16[4,1024,512]{2,1,0:T(8,128)(2,1)} %get-tuple-element.333) | copy-start | bytes 12582916 | tf_op jit(solution)/shard_map/while
  508.7 2.8 copy-start.3
  (8 other events, 15.8 us)
Sparse Core Ops, SparseCore 0:
  185.7 72.3 all-gather.1
where the time goes:
time: 547 us; the launch traced here: 544 us
  other arithmetic  188 us (34%)
  blocking collectives  110 us (20%)
  matrix products  71.5 us (13%)
  local copies, waits for them, and re-layouts  57.2 us (10%)
  waiting for transfers between devices  49.9 us (9%)
  loops' own time  38.1 us (7%)
  starting transfers between devices  15.1 us (3%)
  between operations  14.2 us (3%)
    unnamed x4, other arithmetic  173 us
    all_gather x16, blocking collectives, advance(): curve_groups = lax.all_gather(curve_now[None], 'ccy', axis=0, tiled=True)  88.2 us
    another operation x1, loops' own time, local(): lax.scan(advance, jnp.zeros((), jnp.float32), inputs)  38.1 us
    all_to_all x2, waiting for transfers between devices, cut_exchange(): lax.all_to_all(share, axis, split_axis=0, concat_axis=0, tiled=True)  32.8 us
    dot_general x16, matrix products, advance(): lax.dot_general(slopes, cash_table, (((1,), (1,)), ((), ())), preferred_e...  29.3 us
    all_to_all x1, blocking collectives, from_everyone(): return lax.all_to_all(copies, axis, split_axis=0, concat_axis=0, tiled=True)  21.5 us
    dot_general x16, matrix products, advance(): jnp.einsum('gpc,gcs->ps', discount_all.astype(jnp.bfloat16), cash_all, pr...  21.4 us
    dynamic_slice x32, local copies, waits for them, and re-layouts, local(): lax.scan(advance, jnp.zeros((), jnp.float32), inputs)  18.4 us
  transfers between devices with their start and end apart: 3, of which 3 were waited for; matrix products, arithmetic and copies ran while one was open for 1% of the time, Pallas kernels for 0%

commit v1 on v0

v1 whole, which is shorter than its diff:
```python
import functools

import jax
import jax.numpy as jnp
from jax import lax
from jax.experimental import pallas as pl
from jax.experimental.pallas import tpu as pltpu
from jax.sharding import PartitionSpec as P

NODES = 64
CFG = 1024
NSETS = 512
NCF = 16
TRADES = 2048
DATES = 16
HALF = DATES // 2
CHIP_PATHS = 128
TOTAL_PATHS = 8192
SOFTEN = 0.04
CHUNK = 256
CHUNKS = CFG // CHUNK
ROWS = 512
MESH = pl.DeviceIdType.MESH
BF = jnp.bfloat16
F32 = jnp.float32
NT = (((1,), (1,)), ((), ()))
TN = (((0,), (0,)), ((), ()))


def coords():
    ccy = lax.axis_index("ccy")
    path = lax.axis_index("path")
    core = lax.rem(ccy, 2)
    z = lax.rem(path, 2) * 2 + lax.div(ccy, 2)
    x = lax.rem(lax.div(path, 2), 4)
    y = lax.div(path, 8)
    return y, x, z, core


def device(y, x, z, core):
    return (lax.rem(z, 2) * 2 + core, (y * 4 + x) * 2 + lax.div(z, 2))


def chip_index(y, x, z):
    return (y * 4 + x) * 4 + z


def shifted(i, y, x, z):
    b, c, a = lax.div(i, 16), lax.rem(lax.div(i, 4), 4), lax.rem(i, 4)
    return (
        lax.rem(y + a, 4),
        lax.rem(x + a + b, 4),
        lax.rem(z + a + c, 4),
    )


def remote(src, dst, send, recv, target):
    return pltpu.make_async_remote_copy(
        src_ref=src,
        dst_ref=dst,
        send_sem=send,
        recv_sem=recv,
        device_id=target,
        device_id_type=MESH,
    )


def exchange_kernel(
    slot_ref, store, idx_ref, amt_ref, set_ref,
    tables, curves,
    got, keep, give, bidx, bhi, blo, onehot, flows, made,
    a_send, a_recv, own_sem, p_send, p_recv, l_sem, z_send, z_recv, f_send, f_recv,
    c_send, c_recv,
):
    y, x, z, core = coords()
    group = lax.rem(z, 2) * 2 + core
    partner = device(y, x, z, 1 - core)
    up = device(y, x, lax.rem(z + 1, 4), core)
    down = device(y, x, lax.rem(z + 3, 4), core)
    me = chip_index(y, x, z)

    barrier = pltpu.get_barrier_semaphore()

    def greet(i, carry):
        pl.semaphore_signal(
            barrier, inc=1, device_id=device(*shifted(i, y, x, z), core), device_id_type=MESH
        )
        return carry

    pl.semaphore_signal(barrier, inc=1, device_id=partner, device_id_type=MESH)
    lax.fori_loop(1, 64, greet, 0)
    pl.semaphore_wait(barrier, 64)

    def lanes(chip):
        return pl.ds(pl.multiple_of(chip * CHIP_PATHS, CHIP_PATHS), CHIP_PATHS)

    def curve_copy(i):
        ty, tx, tz = shifted(i, y, x, z)
        return remote(
            store.at[0, :, :, lanes(chip_index(ty, tx, tz))],
            got.at[me],
            a_send.at[i],
            a_recv.at[me],
            device(ty, tx, tz, core),
        )

    def launch(i, carry):
        curve_copy(i).start()
        return carry

    lax.fori_loop(1, 64, launch, 0)
    own_copy = pltpu.make_async_copy(store.at[0, :, :, lanes(me)], got.at[me], own_sem)
    own_copy.start()

    amounts = amt_ref[...]
    indices = idx_ref[...]
    merged = jnp.zeros_like(amounts)
    for k in range(NCF):
        merged = merged + jnp.where(indices == indices[k : k + 1], amounts[k : k + 1], 0.0)
    high = merged.astype(BF).astype(F32)
    low = merged - high
    for k in range(NCF):
        bhi[k] = jnp.broadcast_to(high[k : k + 1], (16, TRADES)).astype(BF)
        blo[k] = jnp.broadcast_to(low[k : k + 1], (16, TRADES)).astype(BF)
    sets = set_ref[...]
    for s in range(0, NSETS, 64):
        ids = lax.broadcasted_iota(jnp.int32, (64, TRADES), 0) + s
        onehot[pl.ds(s, 64), :] = jnp.where(ids == sets, 1.0, 0.0).astype(BF)

    def make_chunk(q, carry):
        base = q * CHUNK
        for k in range(NCF):
            near = jnp.clip(idx_ref[pl.ds(k, 1), :] - base, -1, CHUNK).astype(F32)
            bidx[k] = jnp.broadcast_to(near, (16, TRADES)).astype(BF)

        def spread(t, inner):
            cols = pl.ds(pl.multiple_of(t * 256, 256), 256)
            for sub in range(4):
                ids = (
                    lax.broadcasted_iota(jnp.int32, (4, 16, 256), 0) * 16
                    + lax.broadcasted_iota(jnp.int32, (4, 16, 256), 1)
                    + sub * 64
                ).astype(F32).astype(BF)
                acc_hi = jnp.zeros((4, 16, 256), BF)
                acc_lo = jnp.zeros((4, 16, 256), BF)
                for k in range(NCF):
                    hit = ids == bidx[k, :, cols][None]
                    acc_hi = jnp.where(hit, bhi[k, :, cols][None], acc_hi)
                    acc_lo = jnp.where(hit, blo[k, :, cols][None], acc_lo)
                flows[pl.ds(sub * 64, 64), cols] = acc_hi.reshape(64, 256)
                flows[pl.ds(CHUNK + sub * 64, 64), cols] = acc_lo.reshape(64, 256)
            return inner

        lax.fori_loop(0, TRADES // 256, spread, 0)
        both = lax.dot_general(flows[...], onehot[...], NT, preferred_element_type=F32)
        made[q] = (both[:CHUNK] + both[CHUNK:]).astype(BF)
        return carry

    lax.fori_loop(0, CHUNKS, make_chunk, 0)

    def rows(q):
        return pl.ds(pl.multiple_of(q * CHUNK, CHUNK), CHUNK)

    local = [
        pltpu.make_async_copy(made.at[q], tables.at[group, rows(q), :], l_sem.at[q])
        for q in range(CHUNKS)
    ]
    across = [
        remote(made.at[q], tables.at[group, rows(q), :], z_send.at[q], z_recv.at[q], up if q < 2 else down)
        for q in range(CHUNKS)
    ]
    beside = [
        remote(made.at[q], tables.at[group, rows(q), :], p_send.at[q], p_recv.at[q], partner)
        for q in range(CHUNKS)
    ]
    for q in range(CHUNKS):
        across[q].start()
        beside[q].start()
        local[q].start()

    other = lax.rem(group + 2, 4)
    arriving = [
        remote(made.at[q], tables.at[other, rows(q), :], z_send.at[q], z_recv.at[q], up if q < 2 else down)
        for q in range(CHUNKS)
    ]
    forward = [
        remote(tables.at[other, rows(q), :], tables.at[other, rows(q), :], f_send.at[q], f_recv.at[q], partner)
        for q in range(CHUNKS)
    ]
    for q in (0, 2, 1, 3):
        arriving[q].wait_recv()
        forward[q].start()

    def landed(i, carry):
        curve_copy(i).wait_send()
        ty, tx, tz = shifted(i, y, x, z)
        source = chip_index(ty, tx, tz)
        remote(
            store.at[0, :, :, lanes(me)], got.at[source], a_send.at[i], a_recv.at[source],
            device(ty, tx, tz, core),
        ).wait_recv()
        return carry

    own_copy.wait()
    lax.fori_loop(1, 64, landed, 0)

    def pick(date, low_z):
        slot = slot_ref[date]
        place = lax.div(slot, 2)
        return got[lax.div(place, 2) * 4 + lax.rem(place, 2) * 2 + low_z, lax.rem(slot, 2)]

    for k in range(HALF):
        for low_z in range(2):
            give[low_z, k] = pick((1 - core) * HALF + k, low_z)
            keep[low_z, k] = pick(core * HALF + k, low_z)
    trade = remote(give, curves.at[core], c_send, c_recv, partner)
    trade.start()
    own = pltpu.make_async_copy(keep, curves.at[core], own_sem)
    own.start()
    own.wait()
    trade.wait_send()
    remote(give, curves.at[1 - core], c_send, c_recv, partner).wait_recv()
    for q in range(CHUNKS):
        local[q].wait()
        across[q].wait_send()
        beside[q].wait_send()
        remote(
            made.at[q], tables.at[lax.rem(z, 2) * 2 + 1 - core, rows(q), :], p_send.at[q], p_recv.at[q], partner
        ).wait_recv()
        forward[q].wait_send()
        remote(
            made.at[q], tables.at[lax.rem(z + 1, 2) * 2 + 1 - core, rows(q), :], f_send.at[q], f_recv.at[q], partner
        ).wait_recv()


def exchange(date_slot, curve_store, indices, amounts, sets):
    whole = pl.BlockSpec(memory_space=pltpu.VMEM)
    dma = pltpu.SemaphoreType.DMA
    return pl.pallas_call(
        exchange_kernel,
        out_shape=(
            jax.ShapeDtypeStruct((4, CFG, NSETS), BF),
            jax.ShapeDtypeStruct((2, 2, HALF, NODES, CHIP_PATHS), BF),
        ),
        in_specs=[
            pl.BlockSpec(memory_space=pltpu.SMEM),
            pl.BlockSpec(memory_space=pl.ANY),
            whole,
            whole,
            whole,
        ],
        out_specs=(pl.BlockSpec(memory_space=pl.ANY), pl.BlockSpec(memory_space=pl.ANY)),
        scratch_shapes=[
            pltpu.VMEM((64, 2, NODES, CHIP_PATHS), BF),
            pltpu.VMEM((2, HALF, NODES, CHIP_PATHS), BF),
            pltpu.VMEM((2, HALF, NODES, CHIP_PATHS), BF),
            pltpu.VMEM((NCF, 16, TRADES), BF),
            pltpu.VMEM((NCF, 16, TRADES), BF),
            pltpu.VMEM((NCF, 16, TRADES), BF),
            pltpu.VMEM((NSETS, TRADES), BF),
            pltpu.VMEM((2 * CHUNK, TRADES), BF),
            pltpu.VMEM((CHUNKS, CHUNK, NSETS), BF),
            dma((64,)),
            dma((64,)),
            dma,
            dma((CHUNKS,)),
            dma((CHUNKS,)),
            dma((CHUNKS,)),
            dma((CHUNKS,)),
            dma((CHUNKS,)),
            dma((CHUNKS,)),
            dma((CHUNKS,)),
            dma,
            dma,
        ],
        compiler_params=pltpu.CompilerParams(
            collective_id=0, has_side_effects=True, vmem_limit_bytes=56 * 1024 * 1024
        ),
    )(date_slot, curve_store, indices, amounts, sets)


def grid_tables(date, nodes):
    steps = lax.broadcasted_iota(jnp.int32, (1, CFG), 1) + 1 - 16 * (date + 1)
    steps = steps.astype(F32)
    place = jnp.clip(steps * (1.0 / 16.0), 1.0, float(NODES))
    node = (lax.broadcasted_iota(jnp.int32, (nodes, CFG), 0) + 1).astype(F32)
    weights = jnp.maximum(0.0, 1.0 - jnp.abs(place - node))
    return steps, steps * (1.0 / 32.0), weights


def price_kernel(core_ref, tables, curves, weight_ref, out, discount, value, slope, pull):
    core = core_ref[0]

    def discounts(k, carry):
        steps, remain, weights = grid_tables(core * HALF + k, NODES)
        weights = weights.astype(BF)
        down = remain * -1.0
        live = steps > 0.0
        for g in range(4):
            block = curves[g % 2, g // 2, k]
            rate = lax.dot_general(block, weights, TN, preferred_element_type=F32)
            held = jnp.where(live, jnp.exp(rate * down), 0.0)
            discount[pl.ds(pl.multiple_of(k * CHIP_PATHS, CHIP_PATHS), CHIP_PATHS), pl.ds(g * CFG, CFG)] = (
                held.astype(BF)
            )
        return carry

    lax.fori_loop(0, HALF, discounts, 0)

    per_block = ROWS // CHIP_PATHS

    def block(b, carry):
        span = pl.ds(pl.multiple_of(b * ROWS, ROWS), ROWS)
        value[...] = jnp.zeros_like(value)

        def add_group(g, inner):
            cols = pl.ds(pl.multiple_of(g * CFG, CFG), CFG)
            value[...] += jnp.dot(discount[span, cols], tables[g], preferred_element_type=F32)
            return inner

        lax.fori_loop(0, 4, add_group, 0)
        for i in range(per_block):
            k = b * per_block + i
            v = value[pl.ds(i * CHIP_PATHS, CHIP_PATHS), :]
            square = v * v + SOFTEN
            inverse = lax.rsqrt(square)
            mean = jnp.sum(0.5 * (v + square * inverse), axis=0, keepdims=True) * (1.0 / TOTAL_PATHS)
            scale = weight_ref[pl.ds(k, 1), :] * (0.5 / TOTAL_PATHS)
            slope[pl.ds(i * CHIP_PATHS, CHIP_PATHS), :] = (scale * (1.0 + v * inverse)).astype(BF)
            for part in range(4):
                out[part // 2, part % 2, pl.ds(k, 1), :] = mean[:, part * 128 : (part + 1) * 128]

        def pull_group(n, inner):
            g, c = lax.div(n, CHUNKS), lax.rem(n, CHUNKS)
            cash = tables[g, pl.ds(pl.multiple_of(c * CHUNK, CHUNK), CHUNK), :]
            back = lax.dot_general(slope[...], cash, NT, preferred_element_type=F32)
            cols = pl.ds(pl.multiple_of(n * CHUNK, CHUNK), CHUNK)
            weighed = back * discount[span, cols].astype(F32)
            sums = weighed.reshape(per_block, CHIP_PATHS, CHUNK).sum(axis=1)
            for i in range(per_block):
                pull[b * per_block + i, pl.ds(g, 1), pl.ds(pl.multiple_of(c * CHUNK, CHUNK), CHUNK)] = sums[i : i + 1]
            return inner

        lax.fori_loop(0, 4 * CHUNKS, pull_group, 0)
        return carry

    lax.fori_loop(0, HALF // per_block, block, 0)

    def sensitivities(k, carry):
        _, remain, weights = grid_tables(core * HALF + k, 128)
        weights = weights.astype(BF)
        rest = pull[k] * (remain * -1.0)
        total = jnp.zeros((4, 128), F32)
        for _ in range(3):
            part = rest.astype(BF)
            total = total + lax.dot_general(part, weights, NT, preferred_element_type=F32)
            rest = rest - part.astype(F32)
        for g in range(4):
            out[g // 2, g % 2, pl.ds(HALF + k, 1), :] = total[g : g + 1]
        return carry

    lax.fori_loop(0, HALF, sensitivities, 0)


def price(core, tables, curves, weights):
    whole = pl.BlockSpec(memory_space=pltpu.VMEM)
    paths = HALF * CHIP_PATHS
    return pl.pallas_call(
        price_kernel,
        out_shape=jax.ShapeDtypeStruct((2, 2, 2 * HALF, 128), F32),
        in_specs=[pl.BlockSpec(memory_space=pltpu.SMEM), whole, whole, whole],
        out_specs=whole,
        scratch_shapes=[
            pltpu.VMEM((paths, 4 * CFG), BF),
            pltpu.VMEM((ROWS, NSETS), F32),
            pltpu.VMEM((ROWS, NSETS), BF),
            pltpu.VMEM((HALF, 4, CFG), F32),
        ],
        compiler_params=pltpu.CompilerParams(vmem_limit_bytes=56 * 1024 * 1024),
    )(core, tables, curves, weights)


def total_kernel(
    part, expo, sens, z_buf, y_buf, x_buf, c_buf,
    z_send, z_recv, y_send, y_recv, x_send, x_recv, c_send, c_recv,
):
    y, x, z, core = coords()
    low = lax.rem(z, 2)
    partner = device(y, x, z, 1 - core)
    in_z = [(z + i) % 4 for i in range(1, 4)]
    in_y = [(y + i) % 4 for i in range(1, 4)]
    in_x = [(x + i) % 4 for i in range(1, 4)]
    barrier = pltpu.get_barrier_semaphore()
    targets = (
        [device(y, x, t, core) for t in in_z]
        + [device(t, x, z, core) for t in in_y]
        + [device(y, t, z, core) for t in in_x]
        + [partner]
    )
    for t in targets:
        pl.semaphore_signal(barrier, inc=1, device_id=t, device_id_type=MESH)
    pl.semaphore_wait(barrier, len(targets))

    def stage(source_of, buf, send, recv, here, others, device_of):
        sends = []
        for i, t in enumerate(others):
            copy = remote(source_of(t), buf.at[here], send.at[i], recv.at[here], device_of(t))
            copy.start()
            sends.append(copy)
        for i, t in enumerate(others):
            sends[i].wait_send()
            remote(source_of(here), buf.at[t], send.at[i], recv.at[t], device_of(t)).wait_recv()

    z_buf[z] = part[low]
    stage(
        lambda t: part.at[lax.rem(t, 2)], z_buf, z_send, z_recv, z, in_z,
        lambda t: device(y, x, t, core),
    )
    y_buf[y] = (z_buf[0] + z_buf[1]) + (z_buf[2] + z_buf[3])
    stage(lambda t: y_buf.at[y], y_buf, y_send, y_recv, y, in_y, lambda t: device(t, x, z, core))
    x_buf[x] = (y_buf[0] + y_buf[1]) + (y_buf[2] + y_buf[3])
    stage(lambda t: x_buf.at[x], x_buf, x_send, x_recv, x, in_x, lambda t: device(y, t, z, core))
    c_buf[core] = (x_buf[0] + x_buf[1]) + (x_buf[2] + x_buf[3])
    trade = remote(c_buf.at[core, 1 - core], c_buf.at[core, 1 - core], c_send, c_recv, partner)
    trade.start()
    trade.wait_send()
    remote(c_buf.at[core, core], c_buf.at[1 - core, core], c_send, c_recv, partner).wait_recv()
    for half in range(2):
        block = c_buf[half, core]
        expo[pl.ds(half * HALF, HALF), :] = block[:HALF]
        sens[0, pl.ds(half * HALF, HALF), :] = block[HALF:, :NODES]


def total(part):
    whole = pl.BlockSpec(memory_space=pltpu.VMEM)
    dma = pltpu.SemaphoreType.DMA
    half = (2, 2 * HALF, 128)
    return pl.pallas_call(
        total_kernel,
        out_shape=(
            jax.ShapeDtypeStruct((DATES, NSETS // 4), F32),
            jax.ShapeDtypeStruct((1, DATES, NODES), F32),
        ),
        in_specs=[whole],
        out_specs=(whole, whole),
        scratch_shapes=[
            pltpu.VMEM((4, *half), F32),
            pltpu.VMEM((4, *half), F32),
            pltpu.VMEM((4, *half), F32),
            pltpu.VMEM((2, *half), F32),
            dma((3,)),
            dma((4,)),
            dma((3,)),
            dma((4,)),
            dma((3,)),
            dma((4,)),
            dma,
            dma,
        ],
        compiler_params=pltpu.CompilerParams(collective_id=1, has_side_effects=True),
    )(part)


def local(curve_store, cash_index, cash_amount, trade_set, date_slot, default_weight):
    core = lax.rem(lax.axis_index("ccy"), 2)
    tables, curves = exchange(
        date_slot, curve_store, cash_index[0].T, cash_amount[0].T, trade_set
    )
    weights = lax.dynamic_slice_in_dim(default_weight, core * HALF, HALF, 0)
    part = price(core.reshape(1), tables, curves, weights)
    return total(part)


def solution(mesh):
    in_specs = (
        P("ccy", "path", None, None),
        P("ccy", None, None),
        P("ccy", None, None),
        P("ccy", None),
        P(),
        P(),
    )
    out_specs = (P(None, "ccy"), P("ccy", None, None))
    return jax.shard_map(local, mesh=mesh, in_specs=in_specs, out_specs=out_specs, check_vma=False)
```

time: 547 us -> 102 us (0.19)
  other arithmetic: 188 us -> 0 us
  blocking collectives: 110 us -> 0 us
  Pallas kernels: 0 us -> 96.7 us
  matrix products: 71.5 us -> 0 us
  local copies, waits for them, and re-layouts: 57.2 us -> 3.94 us
  waiting for transfers between devices: 49.9 us -> 0 us
  loops' own time: 38.1 us -> 0 us
  starting transfers between devices: 15.1 us -> 0 us
  between operations: 14.2 us -> 0.67 us
    unnamed x4 -> x0, other arithmetic: 173 us -> none
    pallas_call x0 -> x3, Pallas kernels: none -> 96.7 us  [the longest x1 53.3 us: exchange(): pl.pallas_call(exchange_kernel, out_shape=(jax.ShapeDtypeStruct((4, CFG,...]
    all_gather x16 -> x0, blocking collectives: 88.2 us -> none  [advance(): curve_groups = lax.all_gather(curve_now[None], 'ccy', axis=0, tiled=True)]
    dot_general x64 -> x0, matrix products: 71.5 us -> none  [the longest x16 29.3 us: advance(): lax.dot_general(slopes, cash_table, (((1,), (1,)), ((), ())), preferred_e...]
    another operation x1 -> x0, loops' own time: 38.1 us -> none  [local(): lax.scan(advance, jnp.zeros((), jnp.float32), inputs)]
    all_to_all x2 -> x0, waiting for transfers between devices: 32.8 us -> none  [cut_exchange(): lax.all_to_all(share, axis, split_axis=0, concat_axis=0, tiled=True)]
    dynamic_slice x48 -> x1, local copies, waits for them, and re-layouts: 33.1 us -> 0.6 us  [local(): weights = lax.dynamic_slice_in_dim(default_weight, core * HALF, HALF, 0)]
    all_to_all x1 -> x0, blocking collectives: 21.5 us -> none  [from_everyone(): return lax.all_to_all(copies, axis, split_axis=0, concat_axis=0, tiled=True)]
  transfers between devices with their start and end apart: 3 -> 0, of which waited for: 3 -> 0; matrix products, arithmetic and copies ran while one was open for 1% -> 0% of each run, Pallas kernels for 0% -> 0%
where the time goes in v1:
time: 102 us; the launch traced here: 101 us
  Pallas kernels  96.7 us (95%)
  local copies, waits for them, and re-layouts  3.94 us (4%)
    pallas_call x1, Pallas kernels, exchange(): pl.pallas_call(exchange_kernel, out_shape=(jax.ShapeDtypeStruct((4, CFG,...  53.3 us
    pallas_call x1, Pallas kernels, price(): pl.pallas_call(price_kernel, out_shape=jax.ShapeDtypeStruct((2, 2, 2 * HA...  27.3 us
    pallas_call x1, Pallas kernels, total(): pl.pallas_call(total_kernel, out_shape=(jax.ShapeDtypeStruct((DATES, NSET...  16.1 us
    unnamed x4, local copies, waits for them, and re-layouts  3.34 us

profile of v1, /device:TPU:1, one launch (start us, length us, event | category | flops | bytes accessed | tf_op | source)
XLA Modules:
  0.0 101.3 jit_solution(17939238886689056070)
XLA Ops:
  0.6 0.0 copy-start
  0.7 0.7 copy-done
  1.4 0.6 constant_dynamic-slice_fusion.weight_ref
  2.0 53.3 %shard_map.77 = (bf16[4,1024,512]{2,1,0:T(8,128)(2,1)}, bf16[2,2,8,64,128]{4,3,2,1,0:T(8,128)(2,1)}) custom-call(s32[16]{0:T(128)} %slot_ref.1, bf16[1,2,64,8192]{3,2,1,0:T(8,128)(2,1)} %store.1, s32[16,2048]{1,0:T(8,128)} %bitcast.7, f32[16,2048]{1,0:T(8,128)} %bitcast.8, s32[1,2048]{1,0:T(1,128)} %set_ref.1), custom_call_target="tpu_custom_call" | custom-call | tf_op jit(solution)/shard_map/pallas_call | solution.py:239
  55.3 27.3 %shard_map.78.part = f32[2,2,16,128]{3,2,1,0:T(8,128)} custom-call(s32[1]{0:T(128)} %bitcast.core_ref, bf16[4,1024,512]{2,1,0:T(8,128)(2,1)} %get-tuple-element.4.tables, bf16[2,2,8,64,128]{4,3,2,1,0:T(8,128)(2,1)} %get-tuple-element.5.curves, f32[8,512]{1,0:T(8,128)} %constant_dynamic-slice_fusion.weight_ref), custom_call_target="tpu_custom_call" | custom-call | tf_op jit(solution)/shard_map/pallas_call | solution.py:368
  82.6 16.1 %shard_map.79 = (f32[16,128]{1,0:T(8,128)}, f32[1,16,64]{2,1,0:T(8,128)}) custom-call(f32[2,2,16,128]{3,2,1,0:T(8,128)} %shard_map.78.part), custom_call_target="tpu_custom_call" | custom-call | tf_op jit(solution)/shard_map/pallas_call | solution.py:438
  98.7 1.3 %copy.10 = f32[16,128]{1,0:T(8,128)} copy(f32[16,128]{1,0:T(8,128)} %get-tuple-element.8) | data formatting | bytes 16384
  100.0 1.3 %copy.11 = f32[1,16,64]{2,1,0:T(8,128)} copy(f32[1,16,64]{2,1,0:T(8,128)} %get-tuple-element.9) | data formatting | bytes 8192
Async XLA Ops:
  0.6 0.8 copy-start

commit v2 on v0

v2 whole, which is shorter than its diff:
```python
import jax
import jax.numpy as jnp
from jax import lax
from jax.experimental import pallas as pl
from jax.experimental.pallas import tpu as pltpu
from jax.sharding import PartitionSpec as P

NODES = 64
CFG = 1024
NSETS = 512
NCF = 16
TRADES = 2048
DATES = 16
HALF = DATES // 2
CHIP_PATHS = 128
ROWS = HALF * CHIP_PATHS
TOTAL_PATHS = 8192
SOFTEN = 0.04
LOG2E = 1.4426950408889634
CHUNK = 256
CHUNKS = CFG // CHUNK
TAPS = 24
MESH = pl.DeviceIdType.MESH
BF = jnp.bfloat16
F32 = jnp.float32
NT = (((1,), (1,)), ((), ()))
TN = (((0,), (0,)), ((), ()))


def coords():
    ccy = lax.axis_index("ccy")
    path = lax.axis_index("path")
    core = lax.rem(ccy, 2)
    z = lax.rem(path, 2) * 2 + lax.div(ccy, 2)
    x = lax.rem(lax.div(path, 2), 4)
    y = lax.div(path, 8)
    return y, x, z, core


def device(y, x, z, core):
    return (lax.rem(z, 2) * 2 + core, (y * 4 + x) * 2 + lax.div(z, 2))


def chip_index(y, x, z):
    return (y * 4 + x) * 4 + z


def shifted(i, y, x, z):
    b, c, a = lax.div(i, 16), lax.rem(lax.div(i, 4), 4), lax.rem(i, 4)
    return (
        lax.rem(y + a, 4),
        lax.rem(x + a + b, 4),
        lax.rem(z + a + c, 4),
    )


def remote(src, dst, send, recv, target):
    return pltpu.make_async_remote_copy(
        src_ref=src,
        dst_ref=dst,
        send_sem=send,
        recv_sem=recv,
        device_id=target,
        device_id_type=MESH,
    )


def aligned(start, size):
    return pl.ds(pl.multiple_of(start, size), size)


def grid_tables(date, nodes):
    steps = lax.broadcasted_iota(jnp.int32, (1, CFG), 1) + 1 - 16 * (date + 1)
    steps = steps.astype(F32)
    place = jnp.clip(steps * (1.0 / 16.0), 1.0, float(NODES))
    node = (lax.broadcasted_iota(jnp.int32, (nodes, CFG), 0) + 1).astype(F32)
    weights = jnp.maximum(0.0, 1.0 - jnp.abs(place - node))
    return steps, steps * (1.0 / 32.0), weights


def build_table(raw_i, raw_a, j, slot, tables, bidx, bhi, blo, onehot, flows, send_chunk):
    amounts = raw_a[j]
    indices = raw_i[j, pl.ds(0, NCF), :]
    merged = jnp.zeros_like(amounts)
    for k in range(NCF):
        merged = merged + jnp.where(indices == indices[k : k + 1], amounts[k : k + 1], 0.0)
    high = merged.astype(BF).astype(F32)
    low = merged - high
    for k in range(NCF):
        bhi[k] = jnp.broadcast_to(high[k : k + 1], (16, TRADES)).astype(BF)
        blo[k] = jnp.broadcast_to(low[k : k + 1], (16, TRADES)).astype(BF)
    sets = raw_i[j, pl.ds(NCF, 1), :]
    for s in range(0, NSETS, 64):
        ids = lax.broadcasted_iota(jnp.int32, (64, TRADES), 0) + s
        onehot[pl.ds(s, 64), :] = jnp.where(ids == sets, 1.0, 0.0).astype(BF)

    def make_chunk(q, carry):
        base = q * CHUNK
        for k in range(NCF):
            near = jnp.clip(raw_i[j, pl.ds(k, 1), :] - base, -1, CHUNK).astype(F32)
            bidx[k] = jnp.broadcast_to(near, (16, TRADES)).astype(BF)

        def spread(t, inner):
            cols = aligned(t * 128, 128)
            where = [bidx[k, :, cols] for k in range(NCF)]
            tops = [bhi[k, :, cols] for k in range(NCF)]
            lows = [blo[k, :, cols] for k in range(NCF)]
            for sub in range(CHUNK // 32):
                ids = (
                    lax.broadcasted_iota(jnp.int32, (2, 16, 128), 0) * 16
                    + lax.broadcasted_iota(jnp.int32, (2, 16, 128), 1)
                    + sub * 32
                ).astype(F32).astype(BF)
                acc_hi = jnp.zeros((2, 16, 128), BF)
                acc_lo = jnp.zeros((2, 16, 128), BF)
                for k in range(NCF):
                    hit = ids == where[k][None]
                    acc_hi = jnp.where(hit, tops[k][None], acc_hi)
                    acc_lo = jnp.where(hit, lows[k][None], acc_lo)
                flows[pl.ds(sub * 32, 32), cols] = acc_hi.reshape(32, 128)
                flows[pl.ds(CHUNK + sub * 32, 32), cols] = acc_lo.reshape(32, 128)
            return inner

        lax.fori_loop(0, TRADES // 128, spread, 0)
        both = lax.dot_general(flows[...], onehot[...], NT, preferred_element_type=F32)
        tables[slot, aligned(q * CHUNK, CHUNK), :] = (both[:CHUNK] + both[CHUNK:]).astype(BF)
        send_chunk(q)
        return carry

    lax.fori_loop(0, CHUNKS, make_chunk, 0)


def price(core, tables, curves, weight_ref, part, discount, value, slope, pull, mesh_w):
    for k in range(HALF):
        pull[k] = jnp.zeros((8, CFG), F32)
    part[...] = jnp.zeros_like(part)

    def discounts(k, carry):
        steps, remain, weights = grid_tables(core * HALF + k, NODES)
        weights = weights.astype(BF)
        mesh_w[k] = weights
        down = remain * -LOG2E
        live = steps[:, :256] > 0.0
        for g in range(4):
            rate = lax.dot_general(curves[g % 2, g // 2, k], weights, TN, preferred_element_type=F32)
            held = jnp.exp2(rate * down)
            rows = aligned(k * CHIP_PATHS, CHIP_PATHS)
            discount[rows, pl.ds(g * CFG, 256)] = jnp.where(live, held[:, :256], 0.0).astype(BF)
            discount[rows, pl.ds(g * CFG + 256, CFG - 256)] = held[:, 256:].astype(BF)
        return carry

    lax.fori_loop(0, HALF, discounts, 0)

    value[...] = jnp.dot(discount[:, pl.ds(0, CFG)], tables[0], preferred_element_type=F32)

    def add_group(g, carry):
        value[...] += jnp.dot(discount[:, aligned(g * CFG, CFG)], tables[g], preferred_element_type=F32)
        return carry

    lax.fori_loop(1, 4, add_group, 0)

    def slopes(k, carry):
        rows = aligned(k * CHIP_PATHS, CHIP_PATHS)
        v = value[rows, :]
        square = v * v + SOFTEN
        inverse = lax.rsqrt(square)
        mean = jnp.sum(0.5 * (v + square * inverse), axis=0, keepdims=True) * (1.0 / TOTAL_PATHS)
        scale = weight_ref[pl.ds(core * HALF + k, 1), :] * (0.5 / TOTAL_PATHS)
        slope[rows, :] = (scale * (1.0 + v * inverse)).astype(BF)
        for i in range(4):
            part[i // 2, i % 2, pl.ds(k, 1), :] = mean[:, i * 128 : (i + 1) * 128]
        return carry

    lax.fori_loop(0, HALF, slopes, 0)

    def pull_group(n, carry):
        g, c = lax.div(n, CHUNKS), lax.rem(n, CHUNKS)
        cash = tables[g, aligned(c * CHUNK, CHUNK), :]
        back = lax.dot_general(slope[...], cash, NT, preferred_element_type=F32)
        weighed = back * discount[:, aligned(n * CHUNK, CHUNK)].astype(F32)
        sums = weighed.reshape(HALF, CHIP_PATHS, CHUNK).sum(axis=1)
        for k in range(HALF):
            pull[k, pl.ds(g, 1), aligned(c * CHUNK, CHUNK)] = sums[k : k + 1]
        return carry

    lax.fori_loop(0, 4 * CHUNKS, pull_group, 0)

    for k in range(HALF):
        _, remain, _ = grid_tables(core * HALF + k, 8)
        rest = pull[k] * (remain * -1.0)
        pieces = []
        for _ in range(3):
            piece = rest.astype(BF).astype(F32)
            rest = rest - piece
            pieces.append(piece)
        pieces.append(jnp.zeros_like(rest))
        stack = jnp.concatenate(pieces, axis=0).astype(BF)
        sums = lax.dot_general(stack, mesh_w[k], NT, preferred_element_type=F32)
        total = sums[:8] + sums[8:16] + sums[16:24]
        for g in range(4):
            part[g // 2, g % 2, pl.ds(HALF + k, 1), pl.ds(0, NODES)] = total[g : g + 1]


def kernel(
    slot_ref, store, taps, amounts, weight_ref,
    out,
    got, curves, give, raw_i, raw_a, bidx, bhi, blo, onehot, flows, tables,
    discount, value, slope, pull, mesh_w, part, z_buf, y_buf, x_buf,
    a_send, a_recv, own_sem, l_sem, r_send, r_recv, p_send, p_recv, c_send, c_recv,
    z_send, z_recv, y_send, y_recv, x_send, x_recv,
):
    y, x, z, core = coords()
    low = lax.rem(z, 2)
    group = low * 2 + core
    other = (1 - low) * 2 + core
    partner = device(y, x, z, 1 - core)
    up = device(y, x, lax.rem(z + 1, 4), core)
    down = device(y, x, lax.rem(z + 3, 4), core)
    me = chip_index(y, x, z)
    in_z = [lax.rem(z + i, 4) for i in range(1, 4)]
    in_y = [lax.rem(y + i, 4) for i in range(1, 4)]
    in_x = [lax.rem(x + i, 4) for i in range(1, 4)]

    barrier = pltpu.get_barrier_semaphore()

    def greet(i, carry):
        pl.semaphore_signal(
            barrier, inc=1, device_id=device(*shifted(i, y, x, z), core), device_id_type=MESH
        )
        return carry

    pl.semaphore_signal(barrier, inc=1, device_id=partner, device_id_type=MESH)
    for t in in_x:
        pl.semaphore_signal(barrier, inc=1, device_id=device(y, t, z, 1 - core), device_id_type=MESH)
    lax.fori_loop(1, 64, greet, 0)
    own_raw = [
        pltpu.make_async_copy(taps, raw_i.at[0], l_sem.at[0]),
        pltpu.make_async_copy(amounts, raw_a.at[0], l_sem.at[1]),
    ]
    for copy in own_raw:
        copy.start()
    pl.semaphore_wait(barrier, 67)

    halves = [pl.ds(0, TRADES // 2), pl.ds(TRADES // 2, TRADES // 2)]
    raw = []
    for h, target in enumerate((up, down)):
        raw.append(remote(taps.at[:, halves[h]], raw_i.at[1, :, halves[h]], r_send.at[2 * h], r_recv.at[2 * h], target))
        raw.append(
            remote(amounts.at[:, halves[h]], raw_a.at[1, :, halves[h]], r_send.at[2 * h + 1], r_recv.at[2 * h + 1], target)
        )
    for copy in raw:
        copy.start()

    def lanes(chip):
        return aligned(chip * CHIP_PATHS, CHIP_PATHS)

    def curve_copy(i):
        ty, tx, tz = shifted(i, y, x, z)
        return remote(
            store.at[0, :, :, lanes(chip_index(ty, tx, tz))],
            got.at[me],
            a_send.at[i],
            a_recv.at[me],
            device(ty, tx, tz, core),
        )

    def launch(i, carry):
        curve_copy(i).start()
        return carry

    lax.fori_loop(1, 64, launch, 0)
    own_copy = pltpu.make_async_copy(store.at[0, :, :, lanes(me)], got.at[me], own_sem)
    own_copy.start()

    def table_copy(n, slot, q):
        rows = aligned(q * CHUNK, CHUNK)
        return remote(tables.at[slot, rows, :], tables.at[slot, rows, :], p_send.at[n], p_recv.at[n], partner)

    for copy in own_raw:
        copy.wait()

    def build(j, carry):
        @pl.when(j == 1)
        def _():
            for copy in raw:
                copy.wait()

        slot = lax.rem(low + j, 2) * 2 + core
        build_table(
            raw_i, raw_a, j, slot, tables, bidx, bhi, blo, onehot, flows,
            lambda q: table_copy(j * CHUNKS + q, slot, q).start(),
        )
        return carry

    lax.fori_loop(0, 2, build, 0)

    def landed(i, carry):
        curve_copy(i).wait_send()
        ty, tx, tz = shifted(i, y, x, z)
        source = chip_index(ty, tx, tz)
        remote(
            store.at[0, :, :, lanes(me)], got.at[source], a_send.at[i], a_recv.at[source],
            device(ty, tx, tz, core),
        ).wait_recv()
        return carry

    own_copy.wait()
    lax.fori_loop(1, 64, landed, 0)

    def pick(date, low_z):
        slot = slot_ref[date]
        place = lax.div(slot, 2)
        return got[lax.div(place, 2) * 4 + lax.rem(place, 2) * 2 + low_z, lax.rem(slot, 2)]

    for k in range(HALF):
        for low_z in range(2):
            give[low_z, k] = pick((1 - core) * HALF + k, low_z)
    trade = remote(give, curves.at[core], c_send, c_recv, partner)
    trade.start()
    for k in range(HALF):
        for low_z in range(2):
            curves[core, low_z, k] = pick(core * HALF + k, low_z)
    trade.wait_send()
    remote(give, curves.at[1 - core], c_send, c_recv, partner).wait_recv()
    for j in range(2):
        slot = lax.rem(low + j, 2) * 2 + core
        theirs = lax.rem(low + j, 2) * 2 + 1 - core
        for q in range(CHUNKS):
            table_copy(j * CHUNKS + q, slot, q).wait_send()
            table_copy(j * CHUNKS + q, theirs, q).wait_recv()

    price(core, tables, curves, weight_ref, part, discount, value, slope, pull, mesh_w)

    def stage(source_of, buf, send, recv, here, others, device_of):
        sends = []
        for i, t in enumerate(others):
            copy = remote(source_of(t), buf.at[here], send.at[i], recv.at[here], device_of(t))
            copy.start()
            sends.append(copy)
        for i, t in enumerate(others):
            sends[i].wait_send()
            remote(source_of(here), buf.at[t], send.at[i], recv.at[t], device_of(t)).wait_recv()

    z_buf[z] = part[low]
    stage(
        lambda t: part.at[lax.rem(t, 2)], z_buf, z_send, z_recv, z, in_z,
        lambda t: device(y, x, t, core),
    )
    y_buf[y] = (z_buf[0] + z_buf[1]) + (z_buf[2] + z_buf[3])
    stage(lambda t: y_buf.at[y], y_buf, y_send, y_recv, y, in_y, lambda t: device(t, x, z, core))
    both = (y_buf[0] + y_buf[1]) + (y_buf[2] + y_buf[3])
    give_x = z_buf.at[0]
    give_x[...] = both
    sends = []
    for i, t in enumerate([x] + in_x):
        for c in range(2):
            if i == 0 and c == 0:
                continue
            to_core = lax.rem(core + c, 2)
            copy = remote(
                give_x.at[to_core], x_buf.at[core, x], x_send.at[2 * i + c], x_recv.at[core, x],
                device(y, t, z, to_core),
            )
            copy.start()
            sends.append((copy, t, to_core, 2 * i + c))
    x_buf[core, x] = give_x[core]
    for copy, t, from_core, n in sends:
        copy.wait_send()
        remote(
            give_x.at[core], x_buf.at[from_core, t], x_send.at[n], x_recv.at[from_core, t],
            device(y, t, z, from_core),
        ).wait_recv()
    for half in range(2):
        out[half] = (x_buf[half, 0] + x_buf[half, 1]) + (x_buf[half, 2] + x_buf[half, 3])


def local(curve_store, cash_index, cash_amount, trade_set, date_slot, default_weight):
    taps = jnp.concatenate(
        [cash_index[0].T, trade_set, jnp.zeros((TAPS - NCF - 1, TRADES), jnp.int32)], axis=0
    )
    whole = pl.BlockSpec(memory_space=pltpu.VMEM)
    there = pl.BlockSpec(memory_space=pl.ANY)
    dma = pltpu.SemaphoreType.DMA
    quarter = (2 * HALF, 128)
    sums = pl.pallas_call(
        kernel,
        out_shape=jax.ShapeDtypeStruct((2, *quarter), F32),
        in_specs=[pl.BlockSpec(memory_space=pltpu.SMEM), there, there, there, whole],
        out_specs=whole,
        scratch_shapes=[
            pltpu.VMEM((64, 2, NODES, CHIP_PATHS), BF),
            pltpu.VMEM((2, 2, HALF, NODES, CHIP_PATHS), BF),
            pltpu.VMEM((2, HALF, NODES, CHIP_PATHS), BF),
            pltpu.VMEM((2, TAPS, TRADES), jnp.int32),
            pltpu.VMEM((2, NCF, TRADES), F32),
            pltpu.VMEM((NCF, 16, TRADES), BF),
            pltpu.VMEM((NCF, 16, TRADES), BF),
            pltpu.VMEM((NCF, 16, TRADES), BF),
            pltpu.VMEM((NSETS, TRADES), BF),
            pltpu.VMEM((2 * CHUNK, TRADES), BF),
            pltpu.VMEM((4, CFG, NSETS), BF),
            pltpu.VMEM((ROWS, 4 * CFG), BF),
            pltpu.VMEM((ROWS, NSETS), F32),
            pltpu.VMEM((ROWS, NSETS), BF),
            pltpu.VMEM((HALF, 8, CFG), F32),
            pltpu.VMEM((HALF, NODES, CFG), BF),
            pltpu.VMEM((2, 2, *quarter), F32),
            pltpu.VMEM((4, 2, *quarter), F32),
            pltpu.VMEM((4, 2, *quarter), F32),
            pltpu.VMEM((2, 4, *quarter), F32),
            dma((64,)),
            dma((64,)),
            dma,
            dma((2,)),
            dma((4,)),
            dma((4,)),
            dma((2 * CHUNKS,)),
            dma((2 * CHUNKS,)),
            dma,
            dma,
            dma((3,)),
            dma((4,)),
            dma((3,)),
            dma((4,)),
            dma((8,)),
            dma((2, 4)),
        ],
        compiler_params=pltpu.CompilerParams(
            collective_id=0, has_side_effects=True, vmem_limit_bytes=60 * 1024 * 1024
        ),
    )(date_slot, curve_store, taps, cash_amount[0].T, default_weight)
    exposure = sums[:, :HALF].reshape(DATES, NSETS // 4)
    sens = sums[:, HALF:, :NODES].reshape(1, DATES, NODES)
    return exposure, sens


def solution(mesh):
    in_specs = (
        P("ccy", "path", None, None),
        P("ccy", None, None),
        P("ccy", None, None),
        P("ccy", None),
        P(),
        P(),
    )
    out_specs = (P(None, "ccy"), P("ccy", None, None))
    return jax.shard_map(local, mesh=mesh, in_specs=in_specs, out_specs=out_specs, check_vma=False)
```

time: 547 us -> 95.2 us (0.17)
  other arithmetic: 188 us -> 1.67 us
  blocking collectives: 110 us -> 0 us
  Pallas kernels: 0 us -> 90 us
  matrix products: 71.5 us -> 0 us
  local copies, waits for them, and re-layouts: 57.2 us -> 2.67 us
  waiting for transfers between devices: 49.9 us -> 0 us
  loops' own time: 38.1 us -> 0 us
  starting transfers between devices: 15.1 us -> 0 us
  between operations: 14.2 us -> 0.65 us
    unnamed x4 -> x0, other arithmetic: 173 us -> none
    pallas_call x0 -> x1, Pallas kernels: none -> 90 us  [local(): pl.pallas_call(kernel, out_shape=jax.ShapeDtypeStruct((2, *quarter), F32)...]
    all_gather x16 -> x0, blocking collectives: 88.2 us -> none  [advance(): curve_groups = lax.all_gather(curve_now[None], 'ccy', axis=0, tiled=True)]
    dot_general x64 -> x0, matrix products: 71.5 us -> none  [the longest x16 29.3 us: advance(): lax.dot_general(slopes, cash_table, (((1,), (1,)), ((), ())), preferred_e...]
    another operation x1 -> x0, loops' own time: 38.1 us -> none  [local(): lax.scan(advance, jnp.zeros((), jnp.float32), inputs)]
    dynamic_slice x48 -> x0, local copies, waits for them, and re-layouts: 33.1 us -> none  [the longest x32 18.4 us: local(): lax.scan(advance, jnp.zeros((), jnp.float32), inputs)]
    all_to_all x2 -> x0, waiting for transfers between devices: 32.8 us -> none  [cut_exchange(): lax.all_to_all(share, axis, split_axis=0, concat_axis=0, tiled=True)]
    all_to_all x1 -> x0, blocking collectives: 21.5 us -> none  [from_everyone(): return lax.all_to_all(copies, axis, split_axis=0, concat_axis=0, tiled=True)]
  transfers between devices with their start and end apart: 3 -> 0, of which waited for: 3 -> 0; matrix products, arithmetic and copies ran while one was open for 1% -> 0% of each run, Pallas kernels for 0% -> 0%
where the time goes in v2:
time: 95.2 us; the launch traced here: 95 us
  Pallas kernels  90 us (95%)
  local copies, waits for them, and re-layouts  2.67 us (3%)
  other arithmetic  1.67 us (2%)
    pallas_call x1, Pallas kernels, local(): pl.pallas_call(kernel, out_shape=jax.ShapeDtypeStruct((2, *quarter), F32)...  90 us

profile of v2, /device:TPU:1, one launch (start us, length us, event | category | flops | bytes accessed | tf_op | source)
XLA Modules:
  0.0 95.0 jit_solution(13304224406353667320)
XLA Ops:
  0.6 0.1 pad.2.clone
  0.7 1.7 %add_add_fusion.taps = s32[24,2048]{1,0:T(8,128)} fusion(s32[1,2048]{1,0:T(1,128)} %param.9, s32[16,2048]{1,0:T(8,128)} %bitcast.10, s32[24]{0:T(128)S(1)} %pad.2.clone), kind=kLoop, calls=%fused_computation | loop fusion | flops 98304 | bytes 335968 | tf_op jit(solution)/shard_map/concatenate | solution.py:378
  2.4 90.0 %shard_map.77 = f32[2,16,128]{2,1,0:T(8,128)} custom-call(s32[16]{0:T(128)} %slot_ref.1, bf16[1,2,64,8192]{3,2,1,0:T(8,128)(2,1)} %store.1, s32[24,2048]{1,0:T(8,128)} %add_add_fusion.taps, f32[16,2048]{1,0:T(8,128)} %bitcast.11, f32[16,512]{1,0:T(8,128)} %weight_ref.1), custom_call_target="tpu_custom_call" | custom-call | tf_op jit(solution)/shard_map/pallas_call | solution.py:385
  92.4 1.3 %slice_bitcast_fusion = f32[1,16,64]{2,1,0:T(8,128)} fusion(f32[2,16,128]{2,1,0:T(8,128)} %shard_map.77), kind=kLoop, calls=%fused_computation.1 | loop fusion | bytes 8192 | tf_op jit(solution)/shard_map/reshape | solution.py:433
  93.7 1.3 %slice_bitcast_fusion.1 = f32[16,128]{1,0:T(8,128)} fusion(f32[2,16,128]{2,1,0:T(8,128)} %shard_map.77), kind=kLoop, calls=%fused_computation.2 | loop fusion | bytes 16384 | tf_op jit(solution)/shard_map/reshape | solution.py:432
  (1 shorter events, 0.0 us)

commit v3 on v2

--- a/solution.py
+++ b/solution.py
@@ -78,56 +78,33 @@
     return steps, steps * (1.0 / 32.0), weights
 
 
-def build_table(raw_i, raw_a, j, slot, tables, bidx, bhi, blo, onehot, flows, send_chunk):
+def prepare_trades(raw_i, raw_a, j, merged, onehot):
     amounts = raw_a[j]
     indices = raw_i[j, pl.ds(0, NCF), :]
-    merged = jnp.zeros_like(amounts)
+    sums = jnp.zeros_like(amounts)
     for k in range(NCF):
-        merged = merged + jnp.where(indices == indices[k : k + 1], amounts[k : k + 1], 0.0)
-    high = merged.astype(BF).astype(F32)
-    low = merged - high
-    for k in range(NCF):
-        bhi[k] = jnp.broadcast_to(high[k : k + 1], (16, TRADES)).astype(BF)
-        blo[k] = jnp.broadcast_to(low[k : k + 1], (16, TRADES)).astype(BF)
+        sums = sums + jnp.where(indices == indices[k : k + 1], amounts[k : k + 1], 0.0)
+    merged[j] = sums
     sets = raw_i[j, pl.ds(NCF, 1), :]
     for s in range(0, NSETS, 64):
         ids = lax.broadcasted_iota(jnp.int32, (64, TRADES), 0) + s
-        onehot[pl.ds(s, 64), :] = jnp.where(ids == sets, 1.0, 0.0).astype(BF)
-
-    def make_chunk(q, carry):
-        base = q * CHUNK
+        onehot[j, pl.ds(s, 64), :] = jnp.where(ids == sets, 1.0, 0.0).astype(BF)
+
+
+def spread(raw_i, merged, j, base, start, flows):
+    cols = pl.ds(start, 128)
+    for part in range(0, CHUNK, 128):
+        ids = [lax.broadcasted_iota(jnp.int32, (8, 128), 0) + (base + part + 8 * r) for r in range(16)]
+        accs = [jnp.zeros((8, 128), F32)] * 16
         for k in range(NCF):
-            near = jnp.clip(raw_i[j, pl.ds(k, 1), :] - base, -1, CHUNK).astype(F32)
-            bidx[k] = jnp.broadcast_to(near, (16, TRADES)).astype(BF)
-
-        def spread(t, inner):
-            cols = aligned(t * 128, 128)
-            where = [bidx[k, :, cols] for k in range(NCF)]
-            tops = [bhi[k, :, cols] for k in range(NCF)]
-            lows = [blo[k, :, cols] for k in range(NCF)]
-            for sub in range(CHUNK // 32):
-                ids = (
-                    lax.broadcasted_iota(jnp.int32, (2, 16, 128), 0) * 16
-                    + lax.broadcasted_iota(jnp.int32, (2, 16, 128), 1)
-                    + sub * 32
-                ).astype(F32).astype(BF)
-                acc_hi = jnp.zeros((2, 16, 128), BF)
-                acc_lo = jnp.zeros((2, 16, 128), BF)
-                for k in range(NCF):
-                    hit = ids == where[k][None]
-                    acc_hi = jnp.where(hit, tops[k][None], acc_hi)
-                    acc_lo = jnp.where(hit, lows[k][None], acc_lo)
-                flows[pl.ds(sub * 32, 32), cols] = acc_hi.reshape(32, 128)
-                flows[pl.ds(CHUNK + sub * 32, 32), cols] = acc_lo.reshape(32, 128)
-            return inner
-
-        lax.fori_loop(0, TRADES // 128, spread, 0)
-        both = lax.dot_general(flows[...], onehot[...], NT, preferred_element_type=F32)
-        tables[slot, aligned(q * CHUNK, CHUNK), :] = (both[:CHUNK] + both[CHUNK:]).astype(BF)
-        send_chunk(q)
-        return carry
-
-    lax.fori_loop(0, CHUNKS, make_chunk, 0)
+            where = jnp.broadcast_to(raw_i[j, pl.ds(k, 1), cols], (8, 128))
+            worth = jnp.broadcast_to(merged[j, pl.ds(k, 1), cols], (8, 128))
+            accs = [jnp.where(i == where, worth, acc) for i, acc in zip(ids, accs)]
+        for r in range(0, 16, 2):
+            total = jnp.concatenate(accs[r : r + 2], axis=0)
+            high = total.astype(BF)
+            flows[pl.ds(part + 8 * r, 16), cols] = high
+            flows[pl.ds(CHUNK + part + 8 * r, 16), cols] = (total - high.astype(F32)).astype(BF)
 
 
 def price(core, tables, curves, weight_ref, part, discount, value, slope, pull, mesh_w):
@@ -204,7 +181,7 @@
 def kernel(
     slot_ref, store, taps, amounts, weight_ref,
     out,
-    got, curves, give, raw_i, raw_a, bidx, bhi, blo, onehot, flows, tables,
+    got, curves, give, raw_i, raw_a, merged, onehot, flows, tables,
     discount, value, slope, pull, mesh_w, part, z_buf, y_buf, x_buf,
     a_send, a_recv, own_sem, l_sem, r_send, r_recv, p_send, p_recv, c_send, c_recv,
     z_send, z_recv, y_send, y_recv, x_send, x_recv,
@@ -239,7 +216,9 @@
     ]
     for copy in own_raw:
         copy.start()
-    pl.semaphore_wait(barrier, 67)
+    for copy in own_raw:
+        copy.wait()
+    prepare_trades(raw_i, raw_a, 0, merged, onehot)
 
     halves = [pl.ds(0, TRADES // 2), pl.ds(TRADES // 2, TRADES // 2)]
     raw = []
@@ -248,8 +227,6 @@
         raw.append(
             remote(amounts.at[:, halves[h]], raw_a.at[1, :, halves[h]], r_send.at[2 * h + 1], r_recv.at[2 * h + 1], target)
         )
-    for copy in raw:
-        copy.start()
 
     def lanes(chip):
         return aligned(chip * CHIP_PATHS, CHIP_PATHS)
@@ -268,7 +245,6 @@
         curve_copy(i).start()
         return carry
 
-    lax.fori_loop(1, 64, launch, 0)
     own_copy = pltpu.make_async_copy(store.at[0, :, :, lanes(me)], got.at[me], own_sem)
     own_copy.start()
 
@@ -276,23 +252,35 @@
         rows = aligned(q * CHUNK, CHUNK)
         return remote(tables.at[slot, rows, :], tables.at[slot, rows, :], p_send.at[n], p_recv.at[n], partner)
 
-    for copy in own_raw:
-        copy.wait()
-
-    def build(j, carry):
-        @pl.when(j == 1)
+    def build(n, carry):
+        @pl.when(n == 1)
+        def _():
+            pl.semaphore_wait(barrier, 67)
+            for copy in raw:
+                copy.start()
+            lax.fori_loop(1, 64, launch, 0)
+            table_copy(0, group, 0).start()
+
+        @pl.when(n == CHUNKS)
         def _():
             for copy in raw:
                 copy.wait()
-
+            prepare_trades(raw_i, raw_a, 1, merged, onehot)
+
+        j, q = lax.div(n, CHUNKS), lax.rem(n, CHUNKS)
         slot = lax.rem(low + j, 2) * 2 + core
-        build_table(
-            raw_i, raw_a, j, slot, tables, bidx, bhi, blo, onehot, flows,
-            lambda q: table_copy(j * CHUNKS + q, slot, q).start(),
-        )
-        return carry
-
-    lax.fori_loop(0, 2, build, 0)
+        for t in range(0, TRADES, 128):
+            spread(raw_i, merged, j, q * CHUNK, t, flows)
+        both = lax.dot_general(flows[...], onehot[j], NT, preferred_element_type=F32)
+        tables[slot, aligned(q * CHUNK, CHUNK), :] = (both[:CHUNK] + both[CHUNK:]).astype(BF)
+
+        @pl.when(n > 0)
+        def _():
+            table_copy(n, slot, q).start()
+
+        return carry
+
+    lax.fori_loop(0, 2 * CHUNKS, build, 0)
 
     def landed(i, carry):
         curve_copy(i).wait_send()
@@ -393,10 +381,8 @@
             pltpu.VMEM((2, HALF, NODES, CHIP_PATHS), BF),
             pltpu.VMEM((2, TAPS, TRADES), jnp.int32),
             pltpu.VMEM((2, NCF, TRADES), F32),
-            pltpu.VMEM((NCF, 16, TRADES), BF),
-            pltpu.VMEM((NCF, 16, TRADES), BF),
-            pltpu.VMEM((NCF, 16, TRADES), BF),
-            pltpu.VMEM((NSETS, TRADES), BF),
+            pltpu.VMEM((2, NCF, TRADES), F32),
+            pltpu.VMEM((2, NSETS, TRADES), BF),
             pltpu.VMEM((2 * CHUNK, TRADES), BF),
             pltpu.VMEM((4, CFG, NSETS), BF),
             pltpu.VMEM((ROWS, 4 * CFG), BF),

time: 95.2 us -> 94 us (0.987)
  Pallas kernels: 90 us -> 88.8 us
    pallas_call x1, Pallas kernels: 90 us -> 88.8 us  [local(): pl.pallas_call(kernel, out_shape=jax.ShapeDtypeStruct((2, *quarter), F32)...]
where the time goes in v3:
time: 94 us; the launch traced here: 93.7 us
  Pallas kernels  88.8 us (94%)
  local copies, waits for them, and re-layouts  2.67 us (3%)
  other arithmetic  1.67 us (2%)
    pallas_call x1, Pallas kernels, local(): pl.pallas_call(kernel, out_shape=jax.ShapeDtypeStruct((2, *quarter), F32)...  88.8 us

profile of v3, /device:TPU:1, one launch (start us, length us, event | category | flops | bytes accessed | tf_op | source)
XLA Modules:
  0.0 93.7 jit_solution(7564366294126980495)
XLA Ops:
  0.6 0.1 pad.2.clone
  0.7 1.7 %add_add_fusion.taps = s32[24,2048]{1,0:T(8,128)} fusion(s32[1,2048]{1,0:T(1,128)} %param.9, s32[16,2048]{1,0:T(8,128)} %bitcast.10, s32[24]{0:T(128)S(1)} %pad.2.clone), kind=kLoop, calls=%fused_computation | loop fusion | flops 98304 | bytes 335968 | tf_op jit(solution)/shard_map/concatenate | solution.py:366
  2.4 88.8 %shard_map.77 = f32[2,16,128]{2,1,0:T(8,128)} custom-call(s32[16]{0:T(128)} %slot_ref.1, bf16[1,2,64,8192]{3,2,1,0:T(8,128)(2,1)} %store.1, s32[24,2048]{1,0:T(8,128)} %add_add_fusion.taps, f32[16,2048]{1,0:T(8,128)} %bitcast.11, f32[16,512]{1,0:T(8,128)} %weight_ref.1), custom_call_target="tpu_custom_call" | custom-call | tf_op jit(solution)/shard_map/pallas_call | solution.py:373
  91.1 1.3 %slice_bitcast_fusion = f32[1,16,64]{2,1,0:T(8,128)} fusion(f32[2,16,128]{2,1,0:T(8,128)} %shard_map.77), kind=kLoop, calls=%fused_computation.1 | loop fusion | bytes 8192 | tf_op jit(solution)/shard_map/reshape | solution.py:419
  92.4 1.3 %slice_bitcast_fusion.1 = f32[16,128]{1,0:T(8,128)} fusion(f32[2,16,128]{2,1,0:T(8,128)} %shard_map.77), kind=kLoop, calls=%fused_computation.2 | loop fusion | bytes 16384 | tf_op jit(solution)/shard_map/reshape | solution.py:418
  (1 shorter events, 0.0 us)

commit v4 on v3

--- a/solution.py
+++ b/solution.py
@@ -151,16 +151,16 @@
     lax.fori_loop(0, HALF, slopes, 0)
 
     def pull_group(n, carry):
-        g, c = lax.div(n, CHUNKS), lax.rem(n, CHUNKS)
-        cash = tables[g, aligned(c * CHUNK, CHUNK), :]
+        g, c = lax.div(n, 2), lax.rem(n, 2)
+        cash = tables[g, aligned(c * 512, 512), :]
         back = lax.dot_general(slope[...], cash, NT, preferred_element_type=F32)
-        weighed = back * discount[:, aligned(n * CHUNK, CHUNK)].astype(F32)
-        sums = weighed.reshape(HALF, CHIP_PATHS, CHUNK).sum(axis=1)
+        weighed = back * discount[:, aligned(n * 512, 512)].astype(F32)
+        sums = weighed.reshape(HALF, CHIP_PATHS, 512).sum(axis=1)
         for k in range(HALF):
-            pull[k, pl.ds(g, 1), aligned(c * CHUNK, CHUNK)] = sums[k : k + 1]
-        return carry
-
-    lax.fori_loop(0, 4 * CHUNKS, pull_group, 0)
+            pull[k, pl.ds(g, 1), aligned(c * 512, 512)] = sums[k : k + 1]
+        return carry
+
+    lax.fori_loop(0, 8, pull_group, 0)
 
     for k in range(HALF):
         _, remain, _ = grid_tables(core * HALF + k, 8)
@@ -258,8 +258,11 @@
             pl.semaphore_wait(barrier, 67)
             for copy in raw:
                 copy.start()
+            table_copy(0, group, 0).start()
+
+        @pl.when(n == 2)
+        def _():
             lax.fori_loop(1, 64, launch, 0)
-            table_copy(0, group, 0).start()
 
         @pl.when(n == CHUNKS)
         def _():
@@ -360,6 +363,12 @@
         ).wait_recv()
     for half in range(2):
         out[half] = (x_buf[half, 0] + x_buf[half, 1]) + (x_buf[half, 2] + x_buf[half, 3])
+
+
+def split_kernel(sums, exposure, sens):
+    for half in range(2):
+        exposure[pl.ds(half * HALF, HALF), :] = sums[half, :HALF]
+        sens[0, pl.ds(half * HALF, HALF), :] = sums[half, HALF:, :NODES]
 
 
 def local(curve_store, cash_index, cash_amount, trade_set, date_slot, default_weight):
@@ -415,9 +424,15 @@
             collective_id=0, has_side_effects=True, vmem_limit_bytes=60 * 1024 * 1024
         ),
     )(date_slot, curve_store, taps, cash_amount[0].T, default_weight)
-    exposure = sums[:, :HALF].reshape(DATES, NSETS // 4)
-    sens = sums[:, HALF:, :NODES].reshape(1, DATES, NODES)
-    return exposure, sens
+    return pl.pallas_call(
+        split_kernel,
+        out_shape=(
+            jax.ShapeDtypeStruct((DATES, NSETS // 4), F32),
+            jax.ShapeDtypeStruct((1, DATES, NODES), F32),
+        ),
+        in_specs=[whole],
+        out_specs=(whole, whole),
+    )(sums)
 
 
 def solution(mesh):

time: 94 us -> 78.2 us (0.83)
  Pallas kernels: 88.8 us -> 75.6 us
  local copies, waits for them, and re-layouts: 2.67 us -> 0.08 us
    pallas_call x1, Pallas kernels: 88.8 us -> 74.2 us  [local(): pl.pallas_call(kernel, out_shape=jax.ShapeDtypeStruct((2, *quarter), F32)...]
    reshape x2 -> x0, local copies, waits for them, and re-layouts: 2.59 us -> none  [the longest x1 1.3 us: local(): sens = sums[:, HALF:, :NODES].reshape(1, DATES, NODES)]
    pallas_call x0 -> x1, Pallas kernels: none -> 1.32 us  [local(): pl.pallas_call(split_kernel, out_shape=(jax.ShapeDtypeStruct((DATES, NSET...]
where the time goes in v4:
time: 78.2 us; the launch traced here: 77.9 us
  Pallas kernels  75.6 us (97%)
  other arithmetic  1.67 us (2%)
    pallas_call x1, Pallas kernels, local(): pl.pallas_call(kernel, out_shape=jax.ShapeDtypeStruct((2, *quarter), F32)...  74.2 us
    concatenate x1, other arithmetic, local(): jnp.concatenate([cash_index[0].T, trade_set, jnp.zeros((TAPS - NCF - 1, T...  1.67 us

profile of v4, /device:TPU:1, one launch (start us, length us, event | category | flops | bytes accessed | tf_op | source)
XLA Modules:
  0.0 77.9 jit_solution(13541853174788568152)
XLA Ops:
  0.6 0.1 pad.2.clone
  0.7 1.7 %add_add_fusion.taps = s32[24,2048]{1,0:T(8,128)} fusion(s32[1,2048]{1,0:T(1,128)} %param.9, s32[16,2048]{1,0:T(8,128)} %bitcast.6, s32[24]{0:T(128)S(1)} %pad.2.clone), kind=kLoop, calls=%fused_computation | loop fusion | flops 98304 | bytes 335968 | tf_op jit(solution)/shard_map/concatenate | solution.py:375
  2.4 74.2 %shard_map.77.sums = f32[2,16,128]{2,1,0:T(8,128)} custom-call(s32[16]{0:T(128)} %slot_ref.1, bf16[1,2,64,8192]{3,2,1,0:T(8,128)(2,1)} %store.1, s32[24,2048]{1,0:T(8,128)} %add_add_fusion.taps, f32[16,2048]{1,0:T(8,128)} %bitcast.7, f32[16,512]{1,0:T(8,128)} %weight_ref.1), custom_call_target="tpu_custom_call" | custom-call | tf_op jit(solution)/shard_map/pallas_call | solution.py:382
  76.6 1.3 %shard_map.78 = (f32[16,128]{1,0:T(8,128)}, f32[1,16,64]{2,1,0:T(8,128)}) custom-call(f32[2,16,128]{2,1,0:T(8,128)} %shard_map.77.sums), custom_call_target="tpu_custom_call" | custom-call | tf_op jit(solution)/shard_map/pallas_call | solution.py:427
  (1 shorter events, 0.0 us)

commit v5 on v4

--- a/solution.py
+++ b/solution.py
@@ -66,6 +66,8 @@
 
 
 def aligned(start, size):
+    if isinstance(start, int):
+        return pl.ds(start, size)
     return pl.ds(pl.multiple_of(start, size), size)
 
 
@@ -107,27 +109,26 @@
             flows[pl.ds(CHUNK + part + 8 * r, 16), cols] = (total - high.astype(F32)).astype(BF)
 
 
-def price(core, tables, curves, weight_ref, part, discount, value, slope, pull, mesh_w):
-    for k in range(HALF):
-        pull[k] = jnp.zeros((8, CFG), F32)
-    part[...] = jnp.zeros_like(part)
-
-    def discounts(k, carry):
-        steps, remain, weights = grid_tables(core * HALF + k, NODES)
-        weights = weights.astype(BF)
-        mesh_w[k] = weights
+def store_weights(core, mesh_w):
+    for k in range(HALF):
+        mesh_w[k] = grid_tables(core * HALF + k, NODES)[2].astype(BF)
+
+
+def discounts(core, curves, c, discount, mesh_w):
+    for k in range(HALF):
+        steps, remain, _ = grid_tables(core * HALF + k, 8)
         down = remain * -LOG2E
         live = steps[:, :256] > 0.0
-        for g in range(4):
-            rate = lax.dot_general(curves[g % 2, g // 2, k], weights, TN, preferred_element_type=F32)
+        rows = pl.ds(k * CHIP_PATHS, CHIP_PATHS)
+        for low_z in range(2):
+            rate = lax.dot_general(curves[c, low_z, k], mesh_w[k], TN, preferred_element_type=F32)
             held = jnp.exp2(rate * down)
-            rows = aligned(k * CHIP_PATHS, CHIP_PATHS)
-            discount[rows, pl.ds(g * CFG, 256)] = jnp.where(live, held[:, :256], 0.0).astype(BF)
-            discount[rows, pl.ds(g * CFG + 256, CFG - 256)] = held[:, 256:].astype(BF)
-        return carry
-
-    lax.fori_loop(0, HALF, discounts, 0)
-
+            first = (low_z * 2 + c) * CFG
+            discount[rows, aligned(first, 256)] = jnp.where(live, held[:, :256], 0.0).astype(BF)
+            discount[rows, pl.ds(pl.multiple_of(first + 256, 256), CFG - 256)] = held[:, 256:].astype(BF)
+
+
+def price(core, tables, weight_ref, part, discount, value, slope, pull, mesh_w):
     value[...] = jnp.dot(discount[:, pl.ds(0, CFG)], tables[0], preferred_element_type=F32)
 
     def add_group(g, carry):
@@ -295,6 +296,10 @@
         ).wait_recv()
         return carry
 
+    store_weights(core, mesh_w)
+    for k in range(HALF):
+        pull[k] = jnp.zeros((8, CFG), F32)
+    part[...] = jnp.zeros_like(part)
     own_copy.wait()
     lax.fori_loop(1, 64, landed, 0)
 
@@ -311,8 +316,10 @@
     for k in range(HALF):
         for low_z in range(2):
             curves[core, low_z, k] = pick(core * HALF + k, low_z)
+    discounts(core, curves, core, discount, mesh_w)
     trade.wait_send()
     remote(give, curves.at[1 - core], c_send, c_recv, partner).wait_recv()
+    discounts(core, curves, 1 - core, discount, mesh_w)
     for j in range(2):
         slot = lax.rem(low + j, 2) * 2 + core
         theirs = lax.rem(low + j, 2) * 2 + 1 - core
@@ -320,7 +327,7 @@
             table_copy(j * CHUNKS + q, slot, q).wait_send()
             table_copy(j * CHUNKS + q, theirs, q).wait_recv()
 
-    price(core, tables, curves, weight_ref, part, discount, value, slope, pull, mesh_w)
+    price(core, tables, weight_ref, part, discount, value, slope, pull, mesh_w)
 
     def stage(source_of, buf, send, recv, here, others, device_of):
         sends = []

time: 78.2 us -> 75.9 us (0.971)
  Pallas kernels: 75.6 us -> 73.2 us
    pallas_call x1, Pallas kernels: 74.2 us -> 71.9 us  [local(): pl.pallas_call(kernel, out_shape=jax.ShapeDtypeStruct((2, *quarter), F32)...]
where the time goes in v5:
time: 75.9 us; the launch traced here: 75.6 us
  Pallas kernels  73.2 us (96%)
  other arithmetic  1.67 us (2%)
    pallas_call x1, Pallas kernels, local(): pl.pallas_call(kernel, out_shape=jax.ShapeDtypeStruct((2, *quarter), F32)...  71.9 us
    concatenate x1, other arithmetic, local(): jnp.concatenate([cash_index[0].T, trade_set, jnp.zeros((TAPS - NCF - 1, T...  1.67 us

profile of v5, /device:TPU:1, one launch (start us, length us, event | category | flops | bytes accessed | tf_op | source)
XLA Modules:
  0.0 75.6 jit_solution(5434115603920763134)
XLA Ops:
  0.6 0.1 pad.2.clone
  0.7 1.7 %add_add_fusion.taps = s32[24,2048]{1,0:T(8,128)} fusion(s32[1,2048]{1,0:T(1,128)} %param.9, s32[16,2048]{1,0:T(8,128)} %bitcast.6, s32[24]{0:T(128)S(1)} %pad.2.clone), kind=kLoop, calls=%fused_computation | loop fusion | flops 98304 | bytes 335968 | tf_op jit(solution)/shard_map/concatenate | solution.py:382
  2.4 71.9 %shard_map.77.sums = f32[2,16,128]{2,1,0:T(8,128)} custom-call(s32[16]{0:T(128)} %slot_ref.1, bf16[1,2,64,8192]{3,2,1,0:T(8,128)(2,1)} %store.1, s32[24,2048]{1,0:T(8,128)} %add_add_fusion.taps, f32[16,2048]{1,0:T(8,128)} %bitcast.7, f32[16,512]{1,0:T(8,128)} %weight_ref.1), custom_call_target="tpu_custom_call" | custom-call | tf_op jit(solution)/shard_map/pallas_call | solution.py:389
  74.3 1.3 %shard_map.78 = (f32[16,128]{1,0:T(8,128)}, f32[1,16,64]{2,1,0:T(8,128)}) custom-call(f32[2,16,128]{2,1,0:T(8,128)} %shard_map.77.sums), custom_call_target="tpu_custom_call" | custom-call | tf_op jit(solution)/shard_map/pallas_call | solution.py:434
  (1 shorter events, 0.0 us)

commit v6 on v5

--- a/solution.py
+++ b/solution.py
@@ -114,7 +114,8 @@
         mesh_w[k] = grid_tables(core * HALF + k, NODES)[2].astype(BF)
 
 
-def discounts(core, curves, c, discount, mesh_w):
+def discounts(core, curves, h, discount, mesh_w):
+    c = lax.rem(core + h, 2)
     for k in range(HALF):
         steps, remain, _ = grid_tables(core * HALF + k, 8)
         down = remain * -LOG2E
@@ -123,20 +124,12 @@
         for low_z in range(2):
             rate = lax.dot_general(curves[c, low_z, k], mesh_w[k], TN, preferred_element_type=F32)
             held = jnp.exp2(rate * down)
-            first = (low_z * 2 + c) * CFG
+            first = (h * 2 + low_z) * CFG
             discount[rows, aligned(first, 256)] = jnp.where(live, held[:, :256], 0.0).astype(BF)
-            discount[rows, pl.ds(pl.multiple_of(first + 256, 256), CFG - 256)] = held[:, 256:].astype(BF)
+            discount[rows, pl.ds(first + 256, CFG - 256)] = held[:, 256:].astype(BF)
 
 
 def price(core, tables, weight_ref, part, discount, value, slope, pull, mesh_w):
-    value[...] = jnp.dot(discount[:, pl.ds(0, CFG)], tables[0], preferred_element_type=F32)
-
-    def add_group(g, carry):
-        value[...] += jnp.dot(discount[:, aligned(g * CFG, CFG)], tables[g], preferred_element_type=F32)
-        return carry
-
-    lax.fori_loop(1, 4, add_group, 0)
-
     def slopes(k, carry):
         rows = aligned(k * CHIP_PATHS, CHIP_PATHS)
         v = value[rows, :]
@@ -149,19 +142,19 @@
             part[i // 2, i % 2, pl.ds(k, 1), :] = mean[:, i * 128 : (i + 1) * 128]
         return carry
 
-    lax.fori_loop(0, HALF, slopes, 0)
+    lax.fori_loop(0, HALF, slopes, 0, unroll=2)
 
     def pull_group(n, carry):
-        g, c = lax.div(n, 2), lax.rem(n, 2)
-        cash = tables[g, aligned(c * 512, 512), :]
+        i, c = lax.div(n, 2), lax.rem(n, 2)
+        cash = tables[lax.rem(core + lax.div(n, 4), 2), aligned(lax.rem(n, 4) * 512, 512), :]
         back = lax.dot_general(slope[...], cash, NT, preferred_element_type=F32)
         weighed = back * discount[:, aligned(n * 512, 512)].astype(F32)
         sums = weighed.reshape(HALF, CHIP_PATHS, 512).sum(axis=1)
         for k in range(HALF):
-            pull[k, pl.ds(g, 1), aligned(c * 512, 512)] = sums[k : k + 1]
-        return carry
-
-    lax.fori_loop(0, 8, pull_group, 0)
+            pull[k, pl.ds(i, 1), aligned(c * 512, 512)] = sums[k : k + 1]
+        return carry
+
+    lax.fori_loop(0, 8, pull_group, 0, unroll=4)
 
     for k in range(HALF):
         _, remain, _ = grid_tables(core * HALF + k, 8)
@@ -175,8 +168,8 @@
         stack = jnp.concatenate(pieces, axis=0).astype(BF)
         sums = lax.dot_general(stack, mesh_w[k], NT, preferred_element_type=F32)
         total = sums[:8] + sums[8:16] + sums[16:24]
-        for g in range(4):
-            part[g // 2, g % 2, pl.ds(HALF + k, 1), pl.ds(0, NODES)] = total[g : g + 1]
+        for i in range(4):
+            part[i % 2, lax.rem(core + i // 2, 2), pl.ds(HALF + k, 1), pl.ds(0, NODES)] = total[i : i + 1]
 
 
 def kernel(
@@ -189,8 +182,6 @@
 ):
     y, x, z, core = coords()
     low = lax.rem(z, 2)
-    group = low * 2 + core
-    other = (1 - low) * 2 + core
     partner = device(y, x, z, 1 - core)
     up = device(y, x, lax.rem(z + 1, 4), core)
     down = device(y, x, lax.rem(z + 3, 4), core)
@@ -249,9 +240,12 @@
     own_copy = pltpu.make_async_copy(store.at[0, :, :, lanes(me)], got.at[me], own_sem)
     own_copy.start()
 
-    def table_copy(n, slot, q):
-        rows = aligned(q * CHUNK, CHUNK)
-        return remote(tables.at[slot, rows, :], tables.at[slot, rows, :], p_send.at[n], p_recv.at[n], partner)
+    def table_rows(n):
+        return aligned(lax.rem(low + lax.div(n, CHUNKS), 2) * CFG + lax.rem(n, CHUNKS) * CHUNK, CHUNK)
+
+    def table_copy(n, c):
+        block = tables.at[c, table_rows(n), :]
+        return remote(block, block, p_send.at[n], p_recv.at[n], partner)
 
     def build(n, carry):
         @pl.when(n == 1)
@@ -259,7 +253,7 @@
             pl.semaphore_wait(barrier, 67)
             for copy in raw:
                 copy.start()
-            table_copy(0, group, 0).start()
+            table_copy(jnp.int32(0), core).start()
 
         @pl.when(n == 2)
         def _():
@@ -272,15 +266,14 @@
             prepare_trades(raw_i, raw_a, 1, merged, onehot)
 
         j, q = lax.div(n, CHUNKS), lax.rem(n, CHUNKS)
-        slot = lax.rem(low + j, 2) * 2 + core
         for t in range(0, TRADES, 128):
             spread(raw_i, merged, j, q * CHUNK, t, flows)
         both = lax.dot_general(flows[...], onehot[j], NT, preferred_element_type=F32)
-        tables[slot, aligned(q * CHUNK, CHUNK), :] = (both[:CHUNK] + both[CHUNK:]).astype(BF)
+        tables[core, table_rows(n), :] = (both[:CHUNK] + both[CHUNK:]).astype(BF)
 
         @pl.when(n > 0)
         def _():
-            table_copy(n, slot, q).start()
+            table_copy(n, core).start()
 
         return carry
 
@@ -316,16 +309,15 @@
     for k in range(HALF):
         for low_z in range(2):
             curves[core, low_z, k] = pick(core * HALF + k, low_z)
-    discounts(core, curves, core, discount, mesh_w)
+    discounts(core, curves, 0, discount, mesh_w)
     trade.wait_send()
     remote(give, curves.at[1 - core], c_send, c_recv, partner).wait_recv()
-    discounts(core, curves, 1 - core, discount, mesh_w)
-    for j in range(2):
-        slot = lax.rem(low + j, 2) * 2 + core
-        theirs = lax.rem(low + j, 2) * 2 + 1 - core
-        for q in range(CHUNKS):
-            table_copy(j * CHUNKS + q, slot, q).wait_send()
-            table_copy(j * CHUNKS + q, theirs, q).wait_recv()
+    value[...] = jnp.dot(discount[:, pl.ds(0, 2 * CFG)], tables[core], preferred_element_type=F32)
+    discounts(core, curves, 1, discount, mesh_w)
+    for n in range(2 * CHUNKS):
+        table_copy(jnp.int32(n), core).wait_send()
+        table_copy(jnp.int32(n), 1 - core).wait_recv()
+    value[...] += jnp.dot(discount[:, pl.ds(2 * CFG, 2 * CFG)], tables[1 - core], preferred_element_type=F32)
 
     price(core, tables, weight_ref, part, discount, value, slope, pull, mesh_w)
 
@@ -400,7 +392,7 @@
             pltpu.VMEM((2, NCF, TRADES), F32),
             pltpu.VMEM((2, NSETS, TRADES), BF),
             pltpu.VMEM((2 * CHUNK, TRADES), BF),
-            pltpu.VMEM((4, CFG, NSETS), BF),
+            pltpu.VMEM((2, 2 * CFG, NSETS), BF),
             pltpu.VMEM((ROWS, 4 * CFG), BF),
             pltpu.VMEM((ROWS, NSETS), F32),
             pltpu.VMEM((ROWS, NSETS), BF),

time: 75.9 us -> 74.2 us (0.978)
  Pallas kernels: 73.2 us -> 71.5 us
    pallas_call x1, Pallas kernels: 71.9 us -> 70.2 us  [local(): pl.pallas_call(kernel, out_shape=jax.ShapeDtypeStruct((2, *quarter), F32)...]
where the time goes in v6:
time: 74.2 us; the launch traced here: 73.9 us
  Pallas kernels  71.5 us (96%)
  other arithmetic  1.67 us (2%)
    pallas_call x1, Pallas kernels, local(): pl.pallas_call(kernel, out_shape=jax.ShapeDtypeStruct((2, *quarter), F32)...  70.2 us
    concatenate x1, other arithmetic, local(): jnp.concatenate([cash_index[0].T, trade_set, jnp.zeros((TAPS - NCF - 1, T...  1.67 us

profile of v6, /device:TPU:1, one launch (start us, length us, event | category | flops | bytes accessed | tf_op | source)
XLA Modules:
  0.0 73.9 jit_solution(3518771307299096668)
XLA Ops:
  0.6 0.1 pad.2.clone
  0.7 1.7 %add_add_fusion.taps = s32[24,2048]{1,0:T(8,128)} fusion(s32[1,2048]{1,0:T(1,128)} %param.9, s32[16,2048]{1,0:T(8,128)} %bitcast.6, s32[24]{0:T(128)S(1)} %pad.2.clone), kind=kLoop, calls=%fused_computation | loop fusion | flops 98304 | bytes 335968 | tf_op jit(solution)/shard_map/concatenate | solution.py:374
  2.4 70.2 %shard_map.77.sums = f32[2,16,128]{2,1,0:T(8,128)} custom-call(s32[16]{0:T(128)} %slot_ref.1, bf16[1,2,64,8192]{3,2,1,0:T(8,128)(2,1)} %store.1, s32[24,2048]{1,0:T(8,128)} %add_add_fusion.taps, f32[16,2048]{1,0:T(8,128)} %bitcast.7, f32[16,512]{1,0:T(8,128)} %weight_ref.1), custom_call_target="tpu_custom_call" | custom-call | tf_op jit(solution)/shard_map/pallas_call | solution.py:381
  72.6 1.3 %shard_map.78 = (f32[16,128]{1,0:T(8,128)}, f32[1,16,64]{2,1,0:T(8,128)}) custom-call(f32[2,16,128]{2,1,0:T(8,128)} %shard_map.77.sums), custom_call_target="tpu_custom_call" | custom-call | tf_op jit(solution)/shard_map/pallas_call | solution.py:426
  (1 shorter events, 0.0 us)

commit v7 on v6

--- a/solution.py
+++ b/solution.py
@@ -19,7 +19,6 @@
 LOG2E = 1.4426950408889634
 CHUNK = 256
 CHUNKS = CFG // CHUNK
-TAPS = 24
 MESH = pl.DeviceIdType.MESH
 BF = jnp.bfloat16
 F32 = jnp.float32
@@ -80,14 +79,14 @@
     return steps, steps * (1.0 / 32.0), weights
 
 
-def prepare_trades(raw_i, raw_a, j, merged, onehot):
+def prepare_trades(raw_i, raw_a, raw_s, j, merged, onehot):
     amounts = raw_a[j]
-    indices = raw_i[j, pl.ds(0, NCF), :]
+    indices = raw_i[j]
     sums = jnp.zeros_like(amounts)
     for k in range(NCF):
         sums = sums + jnp.where(indices == indices[k : k + 1], amounts[k : k + 1], 0.0)
     merged[j] = sums
-    sets = raw_i[j, pl.ds(NCF, 1), :]
+    sets = raw_s[j]
     for s in range(0, NSETS, 64):
         ids = lax.broadcasted_iota(jnp.int32, (64, TRADES), 0) + s
         onehot[j, pl.ds(s, 64), :] = jnp.where(ids == sets, 1.0, 0.0).astype(BF)
@@ -173,9 +172,9 @@
 
 
 def kernel(
-    slot_ref, store, taps, amounts, weight_ref,
+    slot_ref, store, taps, amounts, sets, weight_ref,
     out,
-    got, curves, give, raw_i, raw_a, merged, onehot, flows, tables,
+    got, curves, give, raw_i, raw_a, raw_s, merged, onehot, flows, tables,
     discount, value, slope, pull, mesh_w, part, z_buf, y_buf, x_buf,
     a_send, a_recv, own_sem, l_sem, r_send, r_recv, p_send, p_recv, c_send, c_recv,
     z_send, z_recv, y_send, y_recv, x_send, x_recv,
@@ -205,20 +204,23 @@
     own_raw = [
         pltpu.make_async_copy(taps, raw_i.at[0], l_sem.at[0]),
         pltpu.make_async_copy(amounts, raw_a.at[0], l_sem.at[1]),
+        pltpu.make_async_copy(sets, raw_s.at[0], l_sem.at[2]),
     ]
     for copy in own_raw:
         copy.start()
     for copy in own_raw:
         copy.wait()
-    prepare_trades(raw_i, raw_a, 0, merged, onehot)
+    prepare_trades(raw_i, raw_a, raw_s, 0, merged, onehot)
 
     halves = [pl.ds(0, TRADES // 2), pl.ds(TRADES // 2, TRADES // 2)]
     raw = []
     for h, target in enumerate((up, down)):
-        raw.append(remote(taps.at[:, halves[h]], raw_i.at[1, :, halves[h]], r_send.at[2 * h], r_recv.at[2 * h], target))
-        raw.append(
-            remote(amounts.at[:, halves[h]], raw_a.at[1, :, halves[h]], r_send.at[2 * h + 1], r_recv.at[2 * h + 1], target)
-        )
+        for i, (mine, there) in enumerate(((taps, raw_i), (amounts, raw_a), (sets, raw_s))):
+            raw.append(
+                remote(
+                    mine.at[:, halves[h]], there.at[1, :, halves[h]], r_send.at[3 * h + i], r_recv.at[3 * h + i], target
+                )
+            )
 
     def lanes(chip):
         return aligned(chip * CHIP_PATHS, CHIP_PATHS)
@@ -263,7 +265,7 @@
         def _():
             for copy in raw:
                 copy.wait()
-            prepare_trades(raw_i, raw_a, 1, merged, onehot)
+            prepare_trades(raw_i, raw_a, raw_s, 1, merged, onehot)
 
         j, q = lax.div(n, CHUNKS), lax.rem(n, CHUNKS)
         for t in range(0, TRADES, 128):
@@ -371,9 +373,6 @@
 
 
 def local(curve_store, cash_index, cash_amount, trade_set, date_slot, default_weight):
-    taps = jnp.concatenate(
-        [cash_index[0].T, trade_set, jnp.zeros((TAPS - NCF - 1, TRADES), jnp.int32)], axis=0
-    )
     whole = pl.BlockSpec(memory_space=pltpu.VMEM)
     there = pl.BlockSpec(memory_space=pl.ANY)
     dma = pltpu.SemaphoreType.DMA
@@ -381,14 +380,15 @@
     sums = pl.pallas_call(
         kernel,
         out_shape=jax.ShapeDtypeStruct((2, *quarter), F32),
-        in_specs=[pl.BlockSpec(memory_space=pltpu.SMEM), there, there, there, whole],
+        in_specs=[pl.BlockSpec(memory_space=pltpu.SMEM), there, there, there, there, whole],
         out_specs=whole,
         scratch_shapes=[
             pltpu.VMEM((64, 2, NODES, CHIP_PATHS), BF),
             pltpu.VMEM((2, 2, HALF, NODES, CHIP_PATHS), BF),
             pltpu.VMEM((2, HALF, NODES, CHIP_PATHS), BF),
-            pltpu.VMEM((2, TAPS, TRADES), jnp.int32),
+            pltpu.VMEM((2, NCF, TRADES), jnp.int32),
             pltpu.VMEM((2, NCF, TRADES), F32),
+            pltpu.VMEM((2, 1, TRADES), jnp.int32),
             pltpu.VMEM((2, NCF, TRADES), F32),
             pltpu.VMEM((2, NSETS, TRADES), BF),
             pltpu.VMEM((2 * CHUNK, TRADES), BF),
@@ -405,9 +405,9 @@
             dma((64,)),
             dma((64,)),
             dma,
-            dma((2,)),
-            dma((4,)),
-            dma((4,)),
+            dma((3,)),
+            dma((6,)),
+            dma((6,)),
             dma((2 * CHUNKS,)),
             dma((2 * CHUNKS,)),
             dma,
@@ -422,7 +422,7 @@
         compiler_params=pltpu.CompilerParams(
             collective_id=0, has_side_effects=True, vmem_limit_bytes=60 * 1024 * 1024
         ),
-    )(date_slot, curve_store, taps, cash_amount[0].T, default_weight)
+    )(date_slot, curve_store, cash_index[0].T, cash_amount[0].T, trade_set, default_weight)
     return pl.pallas_call(
         split_kernel,
         out_shape=(

time: 74.2 us -> 72.5 us (0.977)
  other arithmetic: 1.67 us -> 0 us
    concatenate x1 -> x0, other arithmetic: 1.67 us -> none  [local(): jnp.concatenate([cash_index[0].T, trade_set, jnp.zeros((TAPS - NCF - 1, T...]
where the time goes in v7:
time: 72.5 us; the launch traced here: 72.3 us
  Pallas kernels  71.6 us (99%)
    pallas_call x1, Pallas kernels, local(): pl.pallas_call(kernel, out_shape=jax.ShapeDtypeStruct((2, *quarter), F32)...  70.3 us

profile of v7, /device:TPU:1, one launch (start us, length us, event | category | flops | bytes accessed | tf_op | source)
XLA Modules:
  0.0 72.3 jit_solution(1427998332376410571)
XLA Ops:
  0.6 70.3 %shard_map.77.sums = f32[2,16,128]{2,1,0:T(8,128)} custom-call(s32[16]{0:T(128)} %slot_ref.1, bf16[1,2,64,8192]{3,2,1,0:T(8,128)(2,1)} %store.1, s32[16,2048]{1,0:T(8,128)} %bitcast.6, f32[16,2048]{1,0:T(8,128)} %bitcast.7, s32[1,2048]{1,0:T(1,128)} %sets.1, f32[16,512]{1,0:T(8,128)} %weight_ref.1), custom_call_target="tpu_custom_call" | custom-call | tf_op jit(solution)/shard_map/pallas_call | solution.py:380
  70.9 1.3 %shard_map.78 = (f32[16,128]{1,0:T(8,128)}, f32[1,16,64]{2,1,0:T(8,128)}) custom-call(f32[2,16,128]{2,1,0:T(8,128)} %shard_map.77.sums), custom_call_target="tpu_custom_call" | custom-call | tf_op jit(solution)/shard_map/pallas_call | solution.py:426
